TPU v7x, 128 devices: a whole 4x4x4 slice. The times are simulated.
128 devices in a mesh: pts: 128 (over z, y, x, core).
Axes of the slice: x: 4, y: 4, z: 4, core: 2. Of those that a mesh axis runs over, the one named last changes fastest.
Arguments:
- points: bfloat16 [65536, 64], P('pts'), may hold values from -10 to 10, as said below
- targets: float32 [65536], P('pts'), may hold values from -6 to 6
- ridge_weight: float32 [], replicated, may hold values from 0.5 to 4
Outputs:
- coefficients: float32 [65536], P('pts')
- residual: float32 [65536], P('pts')
Inputs may be any that keep to these rules, and one draw needn't show every extreme that they name: `points`: each point lies near one of 1365 cluster centres; every coordinate is within -10 and 10.
All inputs are finite; a program needn't handle non-finite values.
Results may differ from a plain program's by a relative error of at most 0.005.
Values may be sent and summed in bfloat16 or wider, within the bound.
A program may use at most 192 MiB of HBM per device.

v0:
```python
import functools

import jax
import jax.numpy as jnp
from jax import lax
from jax.experimental import pallas as pl
from jax.experimental.pallas import tpu as pltpu
from jax.sharding import PartitionSpec as P

F32 = jnp.float32
BF16 = jnp.bfloat16
KEEP_BYTES = 40 * 1024 * 1024


def kernel(n, dim, keep, pts_hbm, tgt, ridge, coef_out, res_out, pts, blocks, t_all, w_all,
           c_all, r_a, r_b, kt, sem_in, sem_ps, sem_pr, sem_fs, sem_fr, sem_ws,
           sem_wr, sem_gs, sem_gr, sem_cs, sem_cr):
    me = lax.axis_index("pts")
    half_n = n // 2
    stages = half_n.bit_length() - 1
    local = tgt.shape[1]
    half = local // 2
    quarter = local // 4
    wide = 2 * dim
    t_rows = quarter // wide
    low = half_n // 4

    def device(p, q):
        d = lax.rem(me + p, 2)
        for s in range(stages):
            bit = half_n >> (s if s >= stages - 2 else stages - 3 - s)
            d = d + lax.rem(me // bit + q // (1 << s), 2) * bit
        return d

    def stage_bit(z, s):
        if z and s >= stages - 2:
            s = 2 * stages - 3 - s
        return 1 << s

    def swapped(q):
        return q - low * (lax.rem(q // (2 * low), 2) - lax.rem(q // low, 2))

    def turn(i):
        q = jnp.where(i - 1 < 2 * low, i - 1, i)
        q = jnp.where(i - 2 < low, i - 2, q)
        return jnp.where(i == 0, 0, jnp.where(i == 1, low, jnp.where(i == 2, 2 * low, q)))

    partner = device(1, 0)
    load = pltpu.make_async_copy(pts_hbm, pts, sem_in)
    load.start()
    barrier = pltpu.get_barrier_semaphore()
    for dev in [partner, device(0, 3)] + [device(0, 1 << s) for s in range(stages)]:
        pl.semaphore_signal(barrier, inc=1, device_id=(dev,), device_id_type=pl.DeviceIdType.MESH)

    target = tgt[...]
    t_hi = target.astype(BF16)
    t_rest = target - t_hi.astype(F32)
    t_mid = t_rest.astype(BF16)
    t_lo = (t_rest - t_mid.astype(F32)).astype(BF16)
    parts = [part.astype(F32) for part in (t_hi, t_mid, t_lo)]

    def t_tile(z):
        cut = [part[:, i:i + wide] for part in parts for h in (0, half)
               for i in range(h + z * quarter, h + (z + 1) * quarter, wide)]
        pad = -len(cut) % 16
        return jnp.concatenate(cut + [jnp.zeros((pad, wide), F32)], axis=0).astype(BF16)

    load.wait()
    own = pts[...].astype(F32)
    packed = jnp.concatenate([own[:half], own[half:]], axis=1).astype(BF16)
    for z in (0, 1):
        blocks[0, 0, z, 0:quarter] = packed[z * quarter:(z + 1) * quarter]
        blocks[0, 0, z, quarter:] = t_tile(z)
    own_t = own.T
    s_row = jnp.sum(own_t * own_t, axis=0, keepdims=True) * (-1.0 / dim)
    s_hi = s_row.astype(BF16).astype(F32)
    s_mid = (s_row - s_hi).astype(BF16).astype(F32)
    s_lo = s_row - s_hi - s_mid
    rows = lax.broadcasted_iota(jnp.int32, (dim, local), 0)
    pieces = jnp.where(rows == 0, s_hi, jnp.where(rows == 1, s_mid, jnp.where(rows == 2, s_lo, 0.0)))
    pieces = pieces.astype(BF16)
    scaled = (own_t * (2.0 / dim)).astype(BF16)
    minus = jnp.full((dim, local), -1.0 / dim, BF16)
    r_a[0:dim] = scaled
    r_a[dim:2 * dim] = minus
    r_a[2 * dim:3 * dim] = minus
    r_a[3 * dim:4 * dim] = pieces
    r_b[0:dim] = minus
    r_b[dim:2 * dim] = scaled
    r_b[2 * dim:3 * dim] = pieces
    r_b[3 * dim:4 * dim] = minus

    def send(src, dst, ssem, rsem, dev):
        return pltpu.make_async_remote_copy(
            src_ref=src, dst_ref=dst, send_sem=ssem, recv_sem=rsem,
            device_id=(dev,), device_id_type=pl.DeviceIdType.MESH)

    def w_copy(q):
        return send(w_all.at[0, 0], w_all.at[0, q], sem_ws.at[q], sem_wr.at[q], device(0, q))

    def g_copy(q):
        return send(w_all.at[0, q], w_all.at[1, q], sem_gs.at[q], sem_gr.at[q], partner)

    def c_copy(p, q):
        return send(c_all.at[0, 0], c_all.at[p, q], sem_cs.at[p, q], sem_cr.at[p, q], device(p, q))

    def p_copy(z, q, s):
        to = q + (1 << s)
        return send(blocks.at[0, q, z], blocks.at[0, to, z], sem_ps.at[z, to], sem_pr.at[z, to],
                    device(0, stage_bit(z, s)))

    def p_from(z, q):
        return send(blocks.at[0, 0, z], blocks.at[0, q, z], sem_ps.at[z, q], sem_pr.at[z, q], partner)

    def f_copy(z, q):
        return send(blocks.at[0, q, z], blocks.at[1, q, z], sem_fs.at[z, q], sem_fr.at[z, q], partner)

    def each(fn):
        fn(1, 0)

        @pl.loop(1, half_n)
        def _(q):
            fn(0, q)
            fn(1, q)

    pl.semaphore_wait(barrier, stages + 2)
    for z in (0, 1):
        send(blocks.at[0, 0, z], blocks.at[0, 3, z], sem_ps.at[z, 3], sem_pr.at[z, 3], device(0, 3)).start()
    for s in range(stages):
        for z in (0, 1):
            p_copy(z, 0, s).start()
    for z in (0, 1):
        f_copy(z, 0).start()

    lanes = lax.broadcasted_iota(jnp.int32, (quarter, wide), 1)
    first = lanes < dim
    one = jnp.ones((quarter, wide), BF16)

    def tile(pb):
        f = pb.astype(F32)
        sq = f * f
        hi = sq.astype(BF16)
        lo = (sq - hi.astype(F32)).astype(BF16)
        hi = pltpu.roll(hi.astype(F32), dim, 1).astype(BF16)
        top = jnp.concatenate([jnp.where(first, pb, hi), jnp.where(first, lo, one)], axis=1)
        bot = jnp.concatenate([jnp.where(first, hi, pb), jnp.where(first, one, lo)], axis=1)
        return top, bot

    def at(z, h):
        return pl.ds(h * half + z * quarter, quarter)

    def absorb(p, q, vec_of, acc):
        slots = (q, swapped(q))
        tiles = [tile(blocks[p, q, z, 0:quarter]) for z in (0, 1)]
        vecs = [vec_of(p, q, z, slots[z]) for z in (0, 1)]
        for h in (0, 1):
            both = jnp.concatenate([tiles[0][h], tiles[1][h]], axis=0)
            e = jnp.dot(both, (r_a, r_b)[h][...], preferred_element_type=F32)
            k = jnp.exp(e).astype(BF16)
            if keep:
                for z in (0, 1):
                    kt[p, slots[z], at(z, h)] = k[z * quarter:(z + 1) * quarter]
            v = jnp.concatenate([vecs[0][h], vecs[1][h]], axis=1)
            acc = acc + jnp.dot(v, k, preferred_element_type=F32)
        return acc

    def fresh(p, q, z, slot):
        part = blocks[p, q, z, quarter:].astype(F32)
        found = []
        for h in (0, 1):
            hi, mid, lo = (
                jnp.concatenate([part[(2 * i + h) * t_rows + j:(2 * i + h) * t_rows + j + 1] for j in range(t_rows)], axis=1)
                for i in range(3))
            t_all[p, slot, :, at(z, h)] = hi + mid + lo
            found.append(hi.astype(BF16))
        return found

    def stored(p, q, z, slot):
        return [t_all[p, slot, :, at(z, h)].astype(BF16) for h in (0, 1)]

    acc = absorb(0, 0, fresh, jnp.zeros((1, local), F32))

    def step(i, acc):
        q = turn(i)
        last = turn(i - 1)
        for z in (0, 1):
            p_from(z, q).wait_recv()
            for s in reversed(range(2, stages)):
                @pl.when(q < (1 << s))
                def _():
                    p_copy(z, q, s).start()
            f_copy(z, q).start()
        for z in (0, 1):
            f_copy(z, last).wait_recv()
        acc = absorb(0, q, fresh, acc)
        return absorb(1, last, fresh, acc)

    acc = lax.fori_loop(1, half_n, step, acc)
    for z in (0, 1):
        f_copy(z, half_n - 1).wait_recv()
    acc = absorb(1, half_n - 1, fresh, acc)
    weight = ridge[0, 0]
    w_all[0, 0] = acc + weight * target
    t_whole = t_all[...]
    norm0 = jnp.sum(t_whole * t_whole)
    g_copy(0).start()

    @pl.loop(1, half_n)
    def _(q):
        w_copy(q).start()

    for z in (0, 1):
        f_copy(z, 0).wait_send()

    @pl.loop(1, half_n)
    def _(q):
        for z in (0, 1):
            p_from(z, q).wait_send()
            f_copy(z, q).wait_send()

    @pl.loop(1, half_n)
    def _(q):
        w_copy(q).wait_recv()
        g_copy(q).start()

    @pl.loop(1, half_n)
    def _(q):
        w_copy(q).wait_send()

    @pl.loop(0, half_n)
    def _(q):
        g_copy(q).wait()

    w_whole = w_all[...]
    step0 = norm0 / jnp.sum(t_whole * w_whole)
    r1 = t_whole - step0 * w_whole
    norm1 = jnp.sum(r1 * r1)
    d1 = r1 + (norm1 / norm0) * t_whole
    t_all[...] = d1

    def again(q, acc):
        for p in (0, 1):
            if keep:
                acc = acc + jnp.dot(t_all[p, q].astype(BF16), kt[p, q], preferred_element_type=F32)
            else:
                acc = absorb(p, q, stored, acc)
        return acc

    acc = lax.fori_loop(0, half_n, again, jnp.zeros((1, local), F32))
    d_own = t_all[0, 0]
    applied = acc + weight * d_own
    part = jnp.sum(d_own * applied)
    c_all[0, 0] = jnp.full((1, 128), part, F32)
    each(lambda p, q: c_copy(p, q).start())
    each(lambda p, q: c_copy(p, q).wait_recv())
    each(lambda p, q: c_copy(p, q).wait_send())
    curvature = jnp.sum(jnp.sum(c_all[...], axis=(0, 1)), axis=0, keepdims=True)[:, 0:1]
    step1 = norm1 / curvature
    coef_out[...] = step0 * target + step1 * d_own
    res_out[...] = target - step0 * w_all[0, 0] - step1 * applied


def body(n, points, targets, ridge_weight):
    local, dim = points.shape
    half_n = n // 2
    keep = n * local * local * 2 <= KEEP_BYTES
    kt_shape = (2, half_n, local, local) if keep else (1, 1, 16, 128)
    quarter = local // 4
    t_tile = -(-6 * quarter // (32 * dim)) * 16
    dma = pltpu.SemaphoreType.DMA
    vec = jax.ShapeDtypeStruct((1, local), F32)
    coef, res = pl.pallas_call(
        functools.partial(kernel, n, dim, keep),
        out_shape=(vec, vec),
        in_specs=[
            pl.BlockSpec(memory_space=pl.ANY),
            pl.BlockSpec(memory_space=pltpu.VMEM),
            pl.BlockSpec(memory_space=pltpu.SMEM),
        ],
        out_specs=(pl.BlockSpec(memory_space=pltpu.VMEM), pl.BlockSpec(memory_space=pltpu.VMEM)),
        scratch_shapes=[
            pltpu.VMEM((local, dim), BF16),
            pltpu.VMEM((2, half_n, 2, quarter + t_tile, 2 * dim), BF16),
            pltpu.VMEM((2, half_n, 1, local), F32),
            pltpu.VMEM((2, half_n, 1, local), F32),
            pltpu.VMEM((2, half_n, 1, 128), F32),
            pltpu.VMEM((4 * dim, local), BF16),
            pltpu.VMEM((4 * dim, local), BF16),
            pltpu.VMEM(kt_shape, BF16),
            dma,
            dma((2, half_n)), dma((2, half_n)),
            dma((2, half_n)), dma((2, half_n)),
            dma((half_n,)), dma((half_n,)),
            dma((half_n,)), dma((half_n,)),
            dma((2, half_n)), dma((2, half_n)),
        ],
        compiler_params=pltpu.CompilerParams(
            collective_id=0, has_side_effects=True, vmem_limit_bytes=60 * 1024 * 1024),
    )(points, targets.reshape(1, local), ridge_weight.reshape(1, 1))
    return coef.reshape(local), res.reshape(local)


def solution(mesh):
    n = mesh.shape["pts"]
    return jax.shard_map(
        functools.partial(body, n), mesh=mesh,
        in_specs=(P("pts", None), P("pts"), P()),
        out_specs=(P("pts"), P("pts")), check_vma=False)
```

profile of v0, /device:TPU:1, one launch (start us, length us, event | category | flops | bytes accessed | tf_op | source)
XLA Modules:
  0.0 208.3 jit_solution(7429790967849948591)
XLA Ops:
  1.3 1.6 copy.5.pts_hbm
  2.9 203.6 %shard_map.50 = (f32[1,512]{1,0:T(1,128)}, f32[1,512]{1,0:T(1,128)}) custom-call(bf16[512,64]{1,0:T(8,128)(2,1)} %copy.5.pts_hbm, f32[1,512]{1,0:T(1,128)} %bitcast.5, f32[1,1]{1,0:T(1,128)} %bitcast.4.ridge), custom_call_target="tpu_custom_call" | custom-call | tf_op jit(solution)/shard_map/pallas_call | solution.py:272
  206.4 0.0 copy-start.1
  206.4 0.7 copy-done.1
  207.1 0.0 copy-start
  207.1 0.6 copy.9
  207.7 0.1 copy-done
  207.8 0.6 copy.10
Async XLA Ops:
  206.4 0.7 copy-start.1
  207.1 0.7 copy-start
where the time goes:
time: 209 us; the launch traced here: 208 us
  Pallas kernels  204 us (98%)
  local copies, waits for them, and re-layouts  3.49 us (2%)
    pallas_call x1, Pallas kernels, body(): pl.pallas_call(functools.partial(kernel, n, dim, keep), out_shape=(vec, v...  204 us

commit v1 on v0

v1 whole, which is shorter than its diff:
```python
import functools

import jax
import jax.numpy as jnp
from jax import lax
from jax.experimental import pallas as pl
from jax.experimental.pallas import tpu as pltpu
from jax.sharding import PartitionSpec as P

F32 = jnp.float32
BF16 = jnp.bfloat16
RING = 4
CHIPS = RING ** 3
CUTS = ((0, 80), (80, 80), (160, 96))
PLANE = ((1, 0), (3, 0), (0, 1), (0, 3), (1, 1), (1, 3), (3, 1), (3, 3), (2, 0), (0, 2),
         (1, 2), (3, 2), (2, 1), (2, 3), (2, 2))
FAR = 42


def choose(cond, a, b):
    if isinstance(cond, bool):
        return a if cond else b
    return jnp.where(cond, a, b)


def flip(mu, pos):
    out = 0
    for d in (2, 1, 0):
        out = choose(mu[d] == 2, pos[d] // 2, out)
    for d in (2, 1, 0):
        out = choose(mu[d] % 2 == 1, mu[d] // 2, out)
    return out


def turned(k, m1, m2, m3):
    return ((m3, m2, m1), (m2, m1, m3), (m1, m3, m2))[k]


def dim_of(k, role):
    return ((2, 1, 0), (1, 0, 2), (0, 2, 1))[k][role]


def number(mu):
    return mu[0] * 16 + mu[1] * 4 + mu[2]


def parts(s):
    return s // 16, s // 4 % 4, s % 4


def stage(m1, m2, m3):
    return m3 * 16 + m2 * 4 + m1


def children(m1, m2):
    out = []
    if m2 == 0:
        if m1 == 0:
            out += [((1, 0, 0), 0, 1), ((3, 0, 0), 0, -1)]
        if m1 == 1:
            out += [((2, 0, 0), 0, 1)]
        out += [((m1, 1, 0), 1, 1), ((m1, 3, 0), 1, -1)]
    if m2 == 1 and m1 % 2 == 0:
        out += [((m1, 2, 0), 1, 1)]
    if m2 == 3 and m1 % 2 == 1:
        out += [((m1, 2, 0), 1, -1)]
    return out + [((m1, m2, 1), 2, 1), ((m1, m2, 3), 2, -1)]


def kernel(pts_hbm, tgt, ridge, coef_out, res_out, pts, blocks, tl, t_all, w_all, c_all, qs1, qr1, qs2, qr2,
           r_a, r_b, kt, ka, kb, sem_in, ps, pr, ls, lr, bs, br, ts, tr, ws, wr, cs, cr, q1s, q1r, q2s, q2r):
    me = lax.axis_index("pts")
    local = tgt.shape[1]
    dim = pts.shape[1]
    half = local // 2
    wide = 2 * dim
    core = lax.rem(me, 2)
    chip = me // 2
    pos = (chip // 16, lax.rem(chip // 4, 4), lax.rem(chip, 4))

    def shifted(mu, sign=1):
        return tuple(lax.rem(p + 4 + sign * m, 4) for p, m in zip(pos, mu))

    def device(at, c):
        return number(at) * 2 + lax.rem(c, 2)

    partner = device(pos, core + 1)
    load = pltpu.make_async_copy(pts_hbm, pts, sem_in)
    load.start()
    barrier = pltpu.get_barrier_semaphore()
    near = [partner]
    for d in range(3):
        for sign in (1, -1):
            at = shifted(tuple(int(d == i) for i in range(3)), sign)
            near += [device(at, core), device(at, core + 1)]
    for dev in near:
        pl.semaphore_signal(barrier, inc=1, device_id=(dev,), device_id_type=pl.DeviceIdType.MESH)

    target = tgt[...]
    t_all[0, 0] = target
    low = target.astype(BF16)
    rows2 = jnp.concatenate([low[:, :half].astype(F32), low[:, half:].astype(F32)], axis=0).astype(BF16)
    for k in range(3):
        tl[0, k] = rows2
    qs1[...] = jnp.zeros_like(qs1)
    qs2[...] = jnp.zeros_like(qs2)

    load.wait()
    own = pts[...].astype(F32)
    blocks[0] = jnp.concatenate([own[:half], own[half:]], axis=1).astype(BF16)

    def send(src, dst, ssem, rsem, dev):
        return pltpu.make_async_remote_copy(
            src_ref=src, dst_ref=dst, send_sem=ssem, recv_sem=rsem,
            device_id=(dev,), device_id_type=pl.DeviceIdType.MESH)

    def piece(k, src, to, dev):
        cut = pl.ds(*CUTS[k])
        return (send(blocks.at[src, cut], blocks.at[to, cut], ps.at[k, to], pr.at[k, to], dev),
                send(tl.at[src, k], tl.at[to, k], ls.at[k, to], lr.at[k, to], dev))

    def relay(k, m, to, role, sign):
        d = dim_of(k, role)
        step = tuple(sign if i == d else 0 for i in range(3))
        at = tuple(lax.rem(p + 4 + s, 4) for p, s in zip(pos, step))
        c = core + flip(turned(k, *m), pos) + flip(turned(k, *to), at)
        for copy in piece(k, stage(*m), stage(*to), device(at, c)):
            copy.start()

    def arrive(s):
        for k in range(3):
            for copy in piece(k, 0, s, partner):
                copy.wait_recv()

    def send_on(m1, m2):
        for to, role, sign in children(m1, m2):
            for k in range(3):
                relay(k, (m1, m2, 0), to, role, sign)

    pl.semaphore_wait(barrier, len(near))
    pair = (send(blocks.at[0], blocks.at[CHIPS], bs.at[0], br.at[0], partner),
            send(tl.at[0], tl.at[CHIPS], bs.at[1], br.at[1], partner))
    for copy in pair:
        copy.start()
    send_on(0, 0)

    own_t = own.T
    s_row = jnp.sum(own_t * own_t, axis=0, keepdims=True) * (-1.0 / dim)
    s_hi = s_row.astype(BF16).astype(F32)
    s_mid = (s_row - s_hi).astype(BF16).astype(F32)
    s_lo = s_row - s_hi - s_mid
    rows = lax.broadcasted_iota(jnp.int32, (dim, local), 0)
    pieces = jnp.where(rows == 0, s_hi, jnp.where(rows == 1, s_mid, jnp.where(rows == 2, s_lo, 0.0)))
    pieces = pieces.astype(BF16)
    scaled = (own_t * (2.0 / dim)).astype(BF16)
    minus = jnp.full((dim, local), -1.0 / dim, BF16)
    r_a[0:dim] = scaled
    r_a[dim:2 * dim] = minus
    r_a[2 * dim:3 * dim] = minus
    r_a[3 * dim:4 * dim] = pieces
    r_b[0:dim] = minus
    r_b[dim:2 * dim] = scaled
    r_b[2 * dim:3 * dim] = pieces
    r_b[3 * dim:4 * dim] = minus

    lanes = lax.broadcasted_iota(jnp.int32, (half, wide), 1)
    first = lanes < dim
    one = jnp.ones((half, wide), BF16)

    def form(s, keep):
        pb = blocks[s]
        f = pb.astype(F32)
        sq = f * f
        hi = sq.astype(BF16)
        lo = (sq - hi.astype(F32)).astype(BF16)
        hi = pltpu.roll(hi.astype(F32), dim, 1).astype(BF16)
        top = jnp.concatenate([jnp.where(first, pb, hi), jnp.where(first, lo, one)], axis=1)
        bot = jnp.concatenate([jnp.where(first, hi, pb), jnp.where(first, one, lo)], axis=1)
        for h, lhs, r in ((0, top, r_a), (1, bot, r_b)):
            e = jnp.dot(lhs, r[...], preferred_element_type=F32)
            k = jnp.exp(e).astype(BF16)
            kt[s, h * half:(h + 1) * half] = k
            keep[h * half:(h + 1) * half] = k

    lane2 = lax.broadcasted_iota(jnp.int32, (2, half), 1)
    lane1 = lax.rem(lax.broadcasted_iota(jnp.int32, (1, local), 1), half)

    def by_piece(lane, a, b, c):
        return jnp.where(lane < CUTS[1][0], a, jnp.where(lane < CUTS[2][0], b, c))

    def across(ks, weight):
        found = []
        for k in ks:
            x = k.astype(F32) * weight
            x = (x[:, :128] + x[:, 128:256]) + (x[:, 256:384] + x[:, 384:])
            found.append(jnp.sum(x.T, axis=0, keepdims=True))
        return jnp.concatenate(found, axis=1)

    def share(qs, m, q):
        for k in range(3):
            slot = number(turned(k, *m))
            keep = (lane1 >= CUTS[k][0]) & (lane1 < CUTS[k][0] + CUTS[k][1])
            qs[slot] = jnp.where(keep, q, qs[slot])

    t_low = low.astype(F32)

    def absorb(s, m, held, acc):
        ks = [held[0:half], held[half:]]
        v2 = by_piece(lane2, *(tl[s, k].astype(F32) for k in range(3))).astype(BF16)
        acc = tuple(a + jnp.dot(v2, k, preferred_element_type=F32) for a, k in zip(acc, ks))
        if m is not None:
            share(qs1, m, across(ks, t_low))
        return acc

    zero = jnp.zeros((2, local), F32)
    acc = (zero, zero)
    form(0, ka)
    for copy in pair:
        copy.wait_recv()
    acc = absorb(0, None, ka, acc)
    form(CHIPS, kb)
    here = (CHIPS, None, kb, ka)
    for m1, m2 in PLANE:
        s = stage(m1, m2, 0)
        arrive(s)
        send_on(m1, m2)
        acc = absorb(*here[:3], acc)
        form(s, here[3])
        here = (s, (m1, m2, 0), here[3], here[2])

    k_old, k_new = here[2], here[3]
    last_m = here[1]

    def digit(v):
        return jnp.where(v < 2, v, 5 - v)

    def stage_b(j, acc):
        def place(i, m3):
            return digit(lax.rem(i, 4)), digit(i // 4), m3

        m1, m2, _ = place(j, 0)
        for m3 in (1, 3):
            arrive(stage(m1, m2, m3))
        odd = lax.rem(m1 + m2, 2)
        m3 = 1 + 2 * odd
        for k in range(3):
            d = dim_of(k, 2)
            at = tuple(lax.rem(pos[i] + (5 - 2 * odd if i == d else 4), 4) for i in range(3))
            to = (m1, m2, 2)
            c = core + flip(turned(k, m1, m2, m3), pos) + flip(turned(k, *to), at)
            for copy in piece(k, stage(m1, m2, m3), stage(*to), device(at, c)):
                copy.start()
        p1, p2, p3 = place(j - 1, 3)
        before = tuple(jnp.where(j == 0, a, b) for a, b in zip(last_m, (p1, p2, p3)))
        acc = absorb(stage(*before), before, k_old, acc)
        form(stage(m1, m2, 1), k_new)
        acc = absorb(stage(m1, m2, 1), (m1, m2, 1), k_new, acc)
        form(stage(m1, m2, 3), k_old)
        return acc

    acc = lax.fori_loop(0, 16, stage_b, acc)

    def spread(buf, ssem, rsem, p, e):
        mu = parts(e)
        return send(buf.at[0, 0], buf.at[p, e], ssem.at[p, e], rsem.at[p, e], device(shifted(mu), core + p))

    spread(t_all, ts, tr, 1, 0).start()

    @pl.loop(1, CHIPS)
    def _(e):
        @pl.when(e != FAR)
        def _():
            for p in (0, 1):
                spread(t_all, ts, tr, p, e).start()

    def stage_c(j, acc):
        def place(i):
            return digit(lax.rem(i, 4)), digit(i // 4)

        m1, m2 = place(2 * j)
        n1, n2 = place(2 * j + 1)
        arrive(stage(m1, m2, 2))
        arrive(stage(n1, n2, 2))
        p1, p2 = place(2 * j - 1)
        before = (jnp.where(j == 0, digit(3), p1), jnp.where(j == 0, digit(3), p2), jnp.where(j == 0, 3, 2))
        acc = absorb(stage(*before), before, k_old, acc)
        form(stage(m1, m2, 2), k_new)
        acc = absorb(stage(m1, m2, 2), (m1, m2, 2), k_new, acc)
        form(stage(n1, n2, 2), k_old)
        return acc

    acc = lax.fori_loop(0, 8, stage_c, acc)
    for p in (0, 1):
        spread(t_all, ts, tr, p, FAR).start()
    acc = absorb(stage(2, 2, 2), (2, 2, 2), k_old, acc)

    def q_copy(qs, qr, ssem, rsem, s):
        mu = parts(s)
        return send(qs.at[s], qr.at[s], ssem.at[s], rsem.at[s], device(shifted(mu, -1), core + flip(mu, pos)))

    def others(fn):
        fn(1, 0)

        @pl.loop(1, CHIPS)
        def _(e):
            fn(0, e)
            fn(1, e)

    @pl.loop(1, CHIPS)
    def _(s):
        q_copy(qs1, qr1, q1s, q1r, s).start()

    for copy in pair:
        copy.wait_send()

    @pl.loop(1, CHIPS)
    def _(s):
        for k in range(3):
            for copy in piece(k, 0, s, partner):
                copy.wait_send()

    others(lambda p, e: spread(t_all, ts, tr, p, e).wait_recv())
    others(lambda p, e: spread(t_all, ts, tr, p, e).wait_send())
    t_whole = t_all[...]
    norm0 = jnp.sum(t_whole * t_whole)
    weight = ridge[0, 0]
    base = acc[0][0:1] + acc[1][1:2] + weight * target

    @pl.loop(1, CHIPS)
    def _(s):
        q_copy(qs1, qr1, q1s, q1r, s).wait_recv()

    w_all[0, 0] = base + jnp.sum(qr1[1:CHIPS], axis=0)
    others(lambda p, e: spread(w_all, ws, wr, p, e).start())

    @pl.loop(1, CHIPS)
    def _(s):
        q_copy(qs1, qr1, q1s, q1r, s).wait_send()

    others(lambda p, e: spread(w_all, ws, wr, p, e).wait_recv())
    others(lambda p, e: spread(w_all, ws, wr, p, e).wait_send())

    w_whole = w_all[...]
    step0 = norm0 / jnp.sum(t_whole * w_whole)
    r1 = t_whole - step0 * w_whole
    norm1 = jnp.sum(r1 * r1)
    t_all[...] = r1 + (norm1 / norm0) * t_whole

    d_own = t_all[0, 0]
    d_low = d_own.astype(BF16).astype(F32)

    def again(s, v, acc):
        ks = [kt[s, 0:half], kt[s, half:]]
        vb = v.astype(BF16)
        for h in (0, 1):
            acc = acc + jnp.dot(vb[:, h * half:(h + 1) * half], ks[h], preferred_element_type=F32)
        return acc, ks

    acc = jnp.zeros((1, local), F32)
    acc, _ = again(0, d_own, acc)
    acc, _ = again(CHIPS, t_all[1, 0], acc)

    def second(s, carry):
        acc, curve = carry
        m3, m2, m1 = parts(s)
        found = []
        for k in range(3):
            mu = turned(k, m1, m2, m3)
            found.append(t_all[flip(mu, pos), number(mu)])
        v = by_piece(lane1, *found)
        acc, ks = again(s, v, acc)
        q = across(ks, d_low)
        share(qs2, (m1, m2, m3), q)
        return acc, curve + q * v

    def two(i, carry):
        return second(2 * i + 1, second(2 * i, carry))

    carry = second(1, (acc, jnp.zeros((1, local), F32)))
    acc, curve = lax.fori_loop(1, CHIPS // 2, two, carry)
    applied = acc + weight * d_own
    part = jnp.sum(d_own * applied) + jnp.sum(curve)
    c_all[0, 0] = jnp.full((1, 128), part, F32)

    others(lambda p, e: spread(c_all, cs, cr, p, e).start())

    @pl.loop(1, CHIPS)
    def _(s):
        q_copy(qs2, qr2, q2s, q2r, s).start()

    others(lambda p, e: spread(c_all, cs, cr, p, e).wait_recv())
    others(lambda p, e: spread(c_all, cs, cr, p, e).wait_send())

    @pl.loop(1, CHIPS)
    def _(s):
        q_copy(qs2, qr2, q2s, q2r, s).wait()

    applied = applied + jnp.sum(qr2[1:CHIPS], axis=0)
    curvature = jnp.sum(jnp.sum(c_all[...], axis=(0, 1)), axis=0, keepdims=True)[:, 0:1]
    step1 = norm1 / curvature
    coef_out[...] = step0 * target + step1 * d_own
    res_out[...] = target - step0 * w_all[0, 0] - step1 * applied


def body(points, targets, ridge_weight):
    local, dim = points.shape
    half = local // 2
    dma = pltpu.SemaphoreType.DMA
    vec = jax.ShapeDtypeStruct((1, local), F32)
    rows = pltpu.VMEM((CHIPS, 1, local), F32)
    both = pltpu.VMEM((2, CHIPS, 1, local), F32)
    coef, res = pl.pallas_call(
        kernel,
        out_shape=(vec, vec),
        in_specs=[
            pl.BlockSpec(memory_space=pl.ANY),
            pl.BlockSpec(memory_space=pltpu.VMEM),
            pl.BlockSpec(memory_space=pltpu.SMEM),
        ],
        out_specs=(pl.BlockSpec(memory_space=pltpu.VMEM), pl.BlockSpec(memory_space=pltpu.VMEM)),
        scratch_shapes=[
            pltpu.VMEM((local, dim), BF16),
            pltpu.VMEM((CHIPS + 1, half, 2 * dim), BF16),
            pltpu.VMEM((CHIPS + 1, 3, 2, half), BF16),
            both, both,
            pltpu.VMEM((2, CHIPS, 1, 128), F32),
            rows, rows, rows, rows,
            pltpu.VMEM((4 * dim, local), BF16),
            pltpu.VMEM((4 * dim, local), BF16),
            pltpu.VMEM((CHIPS + 1, local, local), BF16),
            pltpu.VMEM((local, local), BF16),
            pltpu.VMEM((local, local), BF16),
            dma,
            dma((3, CHIPS)), dma((3, CHIPS)),
            dma((3, CHIPS)), dma((3, CHIPS)),
            dma((2,)), dma((2,)),
            dma((2, CHIPS)), dma((2, CHIPS)),
            dma((2, CHIPS)), dma((2, CHIPS)),
            dma((2, CHIPS)), dma((2, CHIPS)),
            dma((CHIPS,)), dma((CHIPS,)),
            dma((CHIPS,)), dma((CHIPS,)),
        ],
        compiler_params=pltpu.CompilerParams(
            collective_id=0, has_side_effects=True, vmem_limit_bytes=62 * 1024 * 1024),
    )(points, targets.reshape(1, local), ridge_weight.reshape(1, 1))
    return coef.reshape(local), res.reshape(local)


def solution(mesh):
    return jax.shard_map(
        body, mesh=mesh,
        in_specs=(P("pts", None), P("pts"), P()),
        out_specs=(P("pts"), P("pts")), check_vma=False)
```

time: 209 us -> 109 us (0.52)
  Pallas kernels: 204 us -> 104 us
    pallas_call x1, Pallas kernels: 204 us -> 104 us  [body(): pl.pallas_call(kernel, out_shape=(vec, vec), in_specs=[pl.BlockSpec(memor...]
where the time goes in v1:
time: 109 us
  Pallas kernels  104 us (95%)
  local copies, waits for them, and re-layouts  3.49 us (3%)
  between operations  1.3 us (1%)
    pallas_call x1, Pallas kernels, body(): pl.pallas_call(kernel, out_shape=(vec, vec), in_specs=[pl.BlockSpec(memor...  104 us
    unnamed x7, local copies, waits for them, and re-layouts  3.49 us

profile of v1, /device:TPU:1, one launch (start us, length us, event | category | flops | bytes accessed | tf_op | source)
XLA Modules:
  0.0 109.2 jit_solution(9427707955402474178)
XLA Ops:
  1.3 1.6 %copy.5.pts_hbm = bf16[512,64]{1,0:T(8,128)(2,1)} copy(bf16[512,64]{0,1:T(8,128)(2,1)} %param.3) | data formatting | bytes 131072 | tf_op args[0]
  2.9 104.4 %shard_map.50 = (f32[1,512]{1,0:T(1,128)}, f32[1,512]{1,0:T(1,128)}) custom-call(bf16[512,64]{1,0:T(8,128)(2,1)} %copy.5.pts_hbm, f32[1,512]{1,0:T(1,128)} %bitcast.5, f32[1,1]{1,0:T(1,128)} %bitcast.4.ridge), custom_call_target="tpu_custom_call" | custom-call | tf_op jit(solution)/shard_map/pallas_call | solution.py:412
  107.2 0.0 copy-start.1
  107.3 0.7 copy-done.1
  107.9 0.0 copy-start
  107.9 0.6 copy.9
  108.5 0.1 copy-done
  108.6 0.6 copy.10
Async XLA Ops:
  107.2 0.7 copy-start.1
  107.9 0.7 copy-start

commit v2 on v1

v2 whole, which is shorter than its diff:
```python
import functools

import jax
import jax.numpy as jnp
from jax import lax
from jax.experimental import pallas as pl
from jax.experimental.pallas import tpu as pltpu
from jax.sharding import PartitionSpec as P

F32 = jnp.float32
BF16 = jnp.bfloat16
RING = 4
CHIPS = RING ** 3
CUTS = ((0, 80), (80, 80), (160, 96))


def reach(m):
    return sum(min(v, RING - v) for v in m)


def ordered():
    every = [(a, b, c) for c in range(RING) for b in range(RING) for a in range(RING) if (a, b, c) != (0, 0, 0)]
    late = (0.0, 0.6, 1.2, 0.6)
    return sorted(every, key=lambda m: (reach(m) + late[m[2]], m[2], m[1] % 2, m[0] % 2, m))


ORDER = [m[2] * 16 + m[1] * 4 + m[0] for m in ordered()]
WORDS = [sum(v * 64 ** n for n, v in enumerate(ORDER[i:i + 5])) for i in range(0, len(ORDER), 5)]


def place(i):
    word = WORDS[-1]
    for n in reversed(range(len(WORDS) - 1)):
        word = jnp.where(i // 5 == n, WORDS[n], word)
    at = lax.rem(i, 5)
    code = word // 64 ** 4
    for n in reversed(range(4)):
        code = jnp.where(at == n, word // 64 ** n % 64, code)
    return code


def choose(cond, a, b):
    if isinstance(cond, bool):
        return a if cond else b
    return jnp.where(cond, a, b)


def flip(mu, pos):
    out = 0
    for d in (2, 1, 0):
        out = choose(mu[d] == 2, pos[d] // 2, out)
    for d in (2, 1, 0):
        out = choose(mu[d] % 2 == 1, mu[d] // 2, out)
    return out


def turned(k, m1, m2, m3):
    return ((m3, m2, m1), (m2, m1, m3), (m1, m3, m2))[k]


def dim_of(k, role):
    return ((2, 1, 0), (1, 0, 2), (0, 2, 1))[k][role]


def number(mu):
    return mu[0] * 16 + mu[1] * 4 + mu[2]


def parts(s):
    return s // 16, s // 4 % 4, s % 4


def far(v):
    return choose(v == 0, 2, choose(v == 3, 0, choose(v == 2, 3, 1)))


def stage(m1, m2, m3):
    return m3 * 16 + m2 * 4 + m1


def kernel(pts_hbm, tgt, ridge, coef_out, res_out, pts, blocks, tl, t_all, w_all, c_all, qs1, qr1, qs2, qr2,
           r_a, r_b, kt, ka, kb, sem_in, pr, lr, sems):
    me = lax.axis_index("pts")
    local = tgt.shape[1]
    dim = pts.shape[0]
    half = local // 2
    wide = 2 * dim
    core = lax.rem(me, 2)
    chip = me // 2
    pos = (chip // 16, lax.rem(chip // 4, 4), lax.rem(chip, 4))

    def shifted(mu, sign=1):
        return tuple(lax.rem(p + 4 + sign * m, 4) for p, m in zip(pos, mu))

    def device(at, c):
        return number(at) * 2 + lax.rem(c, 2)

    partner = device(pos, core + 1)
    load = pltpu.make_async_copy(pts_hbm, pts, sem_in)
    load.start()
    barrier = pltpu.get_barrier_semaphore()
    near = [partner]
    for d in range(3):
        for sign in (1, -1):
            at = shifted(tuple(int(d == i) for i in range(3)), sign)
            near += [device(at, core), device(at, core + 1)]
    for dev in near:
        pl.semaphore_signal(barrier, inc=1, device_id=(dev,), device_id_type=pl.DeviceIdType.MESH)

    target = tgt[...]
    t_all[0] = target
    low = target.astype(BF16)
    rows2 = jnp.concatenate([low[:, :half].astype(F32), low[:, half:].astype(F32)], axis=0).astype(BF16)
    for k in range(3):
        tl[0, k] = rows2
    qs1[...] = jnp.zeros_like(qs1)
    qs2[...] = jnp.zeros_like(qs2)

    load.wait()
    own_t = pts[...].astype(F32)
    own = own_t.T
    blocks[0] = jnp.concatenate([own[:half], own[half:]], axis=1).astype(BF16)

    def send(src, dst, ssem, rsem, dev):
        return pltpu.make_async_remote_copy(
            src_ref=src, dst_ref=dst, send_sem=ssem, recv_sem=rsem,
            device_id=(dev,), device_id_type=pl.DeviceIdType.MESH)

    def piece(k, src, to, dev):
        cut = pl.ds(*CUTS[k])
        return (send(blocks.at[src, cut], blocks.at[to, cut], sems.at[0], pr.at[to], dev),
                send(tl.at[src, k], tl.at[to, k], sems.at[1], lr.at[to], dev))

    def relay(m, to, role, sign):
        for k in range(3):
            d = dim_of(k, role)
            at = tuple(lax.rem(p + 4 + sign, 4) if i == d else p for i, p in enumerate(pos))
            c = core + flip(turned(k, *m), pos) + flip(turned(k, *to), at)
            for copy in piece(k, stage(*m), stage(*to), device(at, c)):
                copy.start()

    def arrive(s):
        send(blocks.at[s], blocks.at[s], sems.at[0], pr.at[s], partner).wait_recv()
        send(tl.at[s], tl.at[s], sems.at[1], lr.at[s], partner).wait_recv()

    def send_on(m1, m2, m3):
        m = (m1, m2, m3)

        @pl.when(m3 == 0)
        def _():
            @pl.when((m1 == 1) & (m2 == 0))
            def _():
                relay((1, 0, 0), (2, 0, 0), 0, 1)

            @pl.when(m2 == 0)
            def _():
                relay((m1, 0, 0), (m1, 1, 0), 1, 1)
                relay((m1, 0, 0), (m1, 3, 0), 1, -1)

            even = lax.rem(m1, 2) == 0

            @pl.when(((m2 == 1) & even) | ((m2 == 3) & (lax.rem(m1, 2) == 1)))
            def _():
                relay((m1, m2, 0), (m1, 2, 0), 1, 2 - m2)

            relay((m1, m2, 0), (m1, m2, 1), 2, 1)
            relay((m1, m2, 0), (m1, m2, 3), 2, -1)

        @pl.when(m3 == 1 + 2 * lax.rem(m1 + m2, 2))
        def _():
            relay(m, (m1, m2, 2), 2, 2 - m3)

    pl.semaphore_wait(barrier, len(near))
    pair = (send(blocks.at[0], blocks.at[CHIPS], sems.at[2], sems.at[3], partner),
            send(tl.at[0], tl.at[CHIPS], sems.at[4], sems.at[5], partner))
    for copy in pair:
        copy.start()
    for role in range(3):
        for to, sign in ((1, 1), (3, -1)):
            relay((0, 0, 0), tuple(to if i == role else 0 for i in range(3)), role, sign)
    s_row = jnp.sum(own_t * own_t, axis=0, keepdims=True) * (-1.0 / dim)
    s_hi = s_row.astype(BF16).astype(F32)
    s_mid = (s_row - s_hi).astype(BF16).astype(F32)
    s_lo = s_row - s_hi - s_mid
    rows = lax.broadcasted_iota(jnp.int32, (dim, local), 0)
    pieces = jnp.where(rows == 0, s_hi, jnp.where(rows == 1, s_mid, jnp.where(rows == 2, s_lo, 0.0)))
    pieces = pieces.astype(BF16)
    scaled = (own_t * (2.0 / dim)).astype(BF16)
    minus = jnp.full((dim, local), -1.0 / dim, BF16)
    r_a[0:dim] = scaled
    r_a[dim:2 * dim] = minus
    r_a[2 * dim:3 * dim] = minus
    r_a[3 * dim:4 * dim] = pieces
    r_b[0:dim] = minus
    r_b[dim:2 * dim] = scaled
    r_b[2 * dim:3 * dim] = pieces
    r_b[3 * dim:4 * dim] = minus

    lanes = lax.broadcasted_iota(jnp.int32, (half, wide), 1)
    first = lanes < dim
    one = jnp.ones((half, wide), BF16)

    def form(s, keep):
        pb = blocks[s]
        f = pb.astype(F32)
        sq = f * f
        hi = sq.astype(BF16)
        lo = (sq - hi.astype(F32)).astype(BF16)
        hi = pltpu.roll(hi.astype(F32), dim, 1).astype(BF16)
        top = jnp.concatenate([jnp.where(first, pb, hi), jnp.where(first, lo, one)], axis=1)
        bot = jnp.concatenate([jnp.where(first, hi, pb), jnp.where(first, one, lo)], axis=1)
        for h, lhs, r in ((0, top, r_a), (1, bot, r_b)):
            e = jnp.dot(lhs, r[...], preferred_element_type=F32)
            k = jnp.exp(e).astype(BF16)
            kt[s, h * half:(h + 1) * half] = k
            keep[h * half:(h + 1) * half] = k

    lane2 = lax.broadcasted_iota(jnp.int32, (2, half), 1)
    lane1 = lax.rem(lax.broadcasted_iota(jnp.int32, (1, local), 1), half)

    def by_piece(lane, a, b, c):
        return jnp.where(lane < CUTS[1][0], a, jnp.where(lane < CUTS[2][0], b, c))

    def across(ks, weight):
        found = []
        for k in ks:
            x = k.astype(F32) * weight
            x = (x[:, :128] + x[:, 128:256]) + (x[:, 256:384] + x[:, 384:])
            found.append(jnp.sum(x.T, axis=0, keepdims=True))
        return jnp.concatenate(found, axis=1)

    def share(qs, m, q):
        for k in range(3):
            slot = number(turned(k, *m))
            keep = (lane1 >= CUTS[k][0]) & (lane1 < CUTS[k][0] + CUTS[k][1])
            qs[slot] = jnp.where(keep, q, qs[slot])

    t_low = low.astype(F32)

    def absorb(s, m, held, acc):
        ks = [held[0:half], held[half:]]
        v2 = by_piece(lane2, *(tl[s, k].astype(F32) for k in range(3))).astype(BF16)
        acc = tuple(a + jnp.dot(v2, k, preferred_element_type=F32) for a, k in zip(acc, ks))
        if m is not None:
            share(qs1, m, across(ks, t_low))
        return acc

    zero = jnp.zeros((2, local), F32)
    acc = (zero, zero)
    form(0, ka)
    for copy in pair:
        copy.wait_recv()
    acc = absorb(0, None, ka, acc)
    form(CHIPS, kb)

    def spread(buf, sem, p, e):
        mu = parts(e)
        return send(buf.at[0], buf.at[p * CHIPS + e], sems.at[sem], sems.at[sem + 1], device(shifted(mu), core + p))

    def gathered(buf, sem):
        rest = buf.at[pl.ds(1, buf.shape[0] - 1)]
        return send(rest, rest, sems.at[sem], sems.at[sem + 1], partner)

    def digits(code):
        m3, m2, m1 = parts(code)
        return m1, m2, m3

    def come(code):
        arrive(code)
        send_on(*digits(code))

    def greet(code):
        mu = turned(0, *digits(code))
        back = number(tuple(lax.rem(4 - v, 4) for v in mu))
        for p in (0, 1):
            spread(t_all, 6, p, back).start()

    spread(t_all, 6, 1, 0).start()

    def two(i, acc):
        a, b = place(2 * i), place(2 * i + 1)
        before = jnp.where(i == 0, 0, place(2 * i - 1))
        come(a)
        come(b)
        acc = absorb(jnp.where(i == 0, CHIPS, before), digits(before), kb, acc)
        form(a, ka)
        greet(a)
        acc = absorb(a, digits(a), ka, acc)
        form(b, kb)
        greet(b)
        return acc

    acc = lax.fori_loop(0, 31, two, acc)
    code = ORDER[62]
    come(code)
    acc = absorb(ORDER[61], digits(ORDER[61]), kb, acc)
    form(code, ka)
    greet(code)
    acc = absorb(code, digits(code), ka, acc)

    def q_copy(qs, qr, sem, s):
        mu = parts(s)
        return send(qs.at[s], qr.at[s], sems.at[sem], sems.at[sem + 1], device(shifted(mu, -1), core + flip(mu, pos)))

    def farthest_first(fn):
        @pl.loop(0, CHIPS - 1)
        def _(i):
            fn(far(i // 16) * 16 + far(i // 4 % 4) * 4 + far(i % 4))

    farthest_first(lambda e: q_copy(qs1, qr1, 8, e).start())
    for copy in pair:
        copy.wait_send()
    gathered(blocks.at[pl.ds(0, CHIPS)], 0).wait_send()
    gathered(tl.at[pl.ds(0, CHIPS)], 1).wait_send()
    gathered(t_all, 6).wait()
    t_whole = t_all[...]
    norm0 = jnp.sum(t_whole * t_whole)
    weight = ridge[0, 0]
    base = acc[0][0:1] + acc[1][1:2] + weight * target
    send(qs1.at[pl.ds(1, CHIPS - 1)], qr1.at[pl.ds(1, CHIPS - 1)], sems.at[8], sems.at[9], partner).wait_recv()
    w_all[0] = base + jnp.sum(qr1[1:CHIPS], axis=0)

    def to_both(buf, sem):
        def both(e):
            for p in (0, 1):
                spread(buf, sem, p, e).start()

        farthest_first(both)
        spread(buf, sem, 1, 0).start()

    to_both(w_all, 10)
    send(qs1.at[pl.ds(1, CHIPS - 1)], qr1.at[pl.ds(1, CHIPS - 1)], sems.at[8], sems.at[9], partner).wait_send()
    gathered(w_all, 10).wait()
    w_whole = w_all[...]
    step0 = norm0 / jnp.sum(t_whole * w_whole)
    r1 = t_whole - step0 * w_whole
    norm1 = jnp.sum(r1 * r1)
    t_all[...] = r1 + (norm1 / norm0) * t_whole

    d_own = t_all[0]
    d_low = d_own.astype(BF16).astype(F32)

    def again(s, v, acc):
        ks = [kt[s, 0:half], kt[s, half:]]
        vb = v.astype(BF16)
        for h in (0, 1):
            acc = acc + jnp.dot(vb[:, h * half:(h + 1) * half], ks[h], preferred_element_type=F32)
        return acc, ks

    acc = jnp.zeros((1, local), F32)
    acc, _ = again(0, d_own, acc)
    acc, _ = again(CHIPS, t_all[CHIPS], acc)

    def second(s, carry):
        acc, curve = carry
        m3, m2, m1 = parts(s)
        found = []
        for k in range(3):
            mu = turned(k, m1, m2, m3)
            found.append(t_all[flip(mu, pos) * CHIPS + number(mu)])
        v = by_piece(lane1, *found)
        acc, ks = again(s, v, acc)
        q = across(ks, d_low)
        share(qs2, (m1, m2, m3), q)
        return acc, curve + q * v

    def next_two(i, carry):
        return second(2 * i + 1, second(2 * i, carry))

    carry = second(1, (acc, jnp.zeros((1, local), F32)))
    acc, curve = lax.fori_loop(1, CHIPS // 2, next_two, carry)
    applied = acc + weight * d_own
    part = jnp.sum(d_own * applied) + jnp.sum(curve)
    c_all[0] = jnp.full((1, 128), part, F32)
    to_both(c_all, 12)
    farthest_first(lambda e: q_copy(qs2, qr2, 14, e).start())
    gathered(c_all, 12).wait()
    send(qs2.at[pl.ds(1, CHIPS - 1)], qr2.at[pl.ds(1, CHIPS - 1)], sems.at[14], sems.at[15], partner).wait()
    applied = applied + jnp.sum(qr2[1:CHIPS], axis=0)
    curvature = jnp.sum(c_all[...], axis=0)[:, 0:1]
    step1 = norm1 / curvature
    coef_out[...] = step0 * target + step1 * d_own
    res_out[...] = target - step0 * w_all[0] - step1 * applied


def body(points, targets, ridge_weight):
    local, dim = points.shape
    half = local // 2
    dma = pltpu.SemaphoreType.DMA
    vec = jax.ShapeDtypeStruct((1, local), F32)
    rows = pltpu.VMEM((CHIPS, 1, local), F32)
    both = pltpu.VMEM((2 * CHIPS, 1, local), F32)
    coef, res = pl.pallas_call(
        kernel,
        out_shape=(vec, vec),
        in_specs=[
            pl.BlockSpec(memory_space=pl.ANY),
            pl.BlockSpec(memory_space=pltpu.VMEM),
            pl.BlockSpec(memory_space=pltpu.SMEM),
        ],
        out_specs=(pl.BlockSpec(memory_space=pltpu.VMEM), pl.BlockSpec(memory_space=pltpu.VMEM)),
        scratch_shapes=[
            pltpu.VMEM((dim, local), BF16),
            pltpu.VMEM((CHIPS + 1, half, 2 * dim), BF16),
            pltpu.VMEM((CHIPS + 1, 3, 2, half), BF16),
            both, both,
            pltpu.VMEM((2 * CHIPS, 1, 128), F32),
            rows, rows, rows, rows,
            pltpu.VMEM((4 * dim, local), BF16),
            pltpu.VMEM((4 * dim, local), BF16),
            pltpu.VMEM((CHIPS + 1, local, local), BF16),
            pltpu.VMEM((local, local), BF16),
            pltpu.VMEM((local, local), BF16),
            dma, dma((CHIPS,)), dma((CHIPS,)), dma((16,)),
        ],
        compiler_params=pltpu.CompilerParams(
            collective_id=0, has_side_effects=True, vmem_limit_bytes=62 * 1024 * 1024),
    )(points.T, targets.reshape(1, local), ridge_weight.reshape(1, 1))
    return coef.reshape(local), res.reshape(local)


def solution(mesh):
    return jax.shard_map(
        body, mesh=mesh,
        in_specs=(P("pts", None), P("pts"), P()),
        out_specs=(P("pts"), P("pts")), check_vma=False)
```

time: 109 us -> 91.6 us (0.84)
  Pallas kernels: 104 us -> 88.2 us
  local copies, waits for them, and re-layouts: 3.49 us -> 1.89 us
    pallas_call x1, Pallas kernels: 104 us -> 88.2 us  [body(): pl.pallas_call(kernel, out_shape=(vec, vec), in_specs=[pl.BlockSpec(memor...]
    unnamed x7 -> x6, local copies, waits for them, and re-layouts: 3.49 us -> 1.89 us
where the time goes in v2:
time: 91.6 us; the launch traced here: 91.3 us
  Pallas kernels  88.2 us (96%)
  local copies, waits for them, and re-layouts  1.89 us (2%)
  between operations  1.29 us (1%)
    pallas_call x1, Pallas kernels, body(): pl.pallas_call(kernel, out_shape=(vec, vec), in_specs=[pl.BlockSpec(memor...  88.2 us
    unnamed x6, local copies, waits for them, and re-layouts  1.89 us

profile of v2, /device:TPU:1, one launch (start us, length us, event | category | flops | bytes accessed | tf_op | source)
XLA Modules:
  0.0 91.3 jit_solution(2424894125332451630)
XLA Ops:
  1.3 88.2 %shard_map.50 = (f32[1,512]{1,0:T(1,128)}, f32[1,512]{1,0:T(1,128)}) custom-call(bf16[64,512]{1,0:T(8,128)(2,1)} %bitcast.6, f32[1,512]{1,0:T(1,128)} %bitcast.7, f32[1,1]{1,0:T(1,128)} %bitcast.5.ridge), custom_call_target="tpu_custom_call" | custom-call | tf_op jit(solution)/shard_map/pallas_call | solution.py:393
  89.4 0.0 copy-start.1
  89.5 0.7 copy-done.1
  90.1 0.0 copy-start
  90.1 0.6 copy.8
  90.7 0.1 copy-done
  90.8 0.6 copy.9
Async XLA Ops:
  89.4 0.7 copy-start.1
  90.1 0.7 copy-start

commit v3 on v0

v3 whole, which is shorter than its diff:
```python
import jax
import jax.numpy as jnp
from jax import lax
from jax.experimental import pallas as pl
from jax.experimental.pallas import tpu as pltpu
from jax.sharding import PartitionSpec as P

F32 = jnp.float32
BF16 = jnp.bfloat16
TREE = (
    ((0, 0, 1), 0, 2, 1), ((0, 1, 0), 0, 1, 1), ((1, 0, 0), 0, 0, 1), ((1, 3, 0), 3, 1, -1), ((1, 1, 0), 2, 0, 1),
    ((3, 0, 1), 1, 0, -1), ((0, 1, 1), 1, 1, 1), ((0, 1, 3), 2, 2, -1), ((1, 0, 1), 3, 2, 1), ((0, 1, 2), 8, 2, -1),
    ((3, 0, 2), 6, 2, 1), ((1, 1, 1), 5, 2, 1), ((1, 2, 0), 4, 1, -1), ((1, 3, 3), 4, 2, -1), ((2, 0, 1), 6, 0, -1),
    ((2, 3, 0), 4, 0, 1), ((0, 2, 1), 7, 1, 1), ((1, 1, 3), 5, 2, -1), ((1, 3, 1), 9, 1, -1), ((1, 2, 1), 12, 1, 1),
    ((1, 2, 3), 13, 2, -1), ((3, 1, 2), 10, 0, -1), ((2, 3, 1), 15, 1, -1), ((2, 3, 3), 14, 0, 1), ((3, 3, 2), 11, 1, -1),
    ((2, 2, 1), 20, 0, 1), ((1, 2, 2), 21, 2, -1), ((2, 1, 2), 22, 0, -1), ((0, 0, 2), 1, 2, 1), ((0, 2, 0), 2, 1, 1),
    ((2, 0, 0), 3, 0, 1), ((0, 2, 2), 10, 1, 1), ((2, 0, 2), 11, 0, -1), ((2, 2, 0), 16, 1, -1), ((2, 2, 2), 26, 2, 1))
PLACES = ((0, 0, 0),) + tuple(t[0] for t in TREE)
SLOTS = len(PLACES)
SELF = 29
UNITS = 2 * SELF + SLOTS - SELF
CHUNKS = ((1, 3), (4, 6), (10, 10), (20, 6), (26, 3), (SELF, SLOTS - SELF))
ALL = tuple((z, y, x) for z in range(4) for y in range(4) for x in range(4))


def chunk_of(s):
    return [lo <= s < lo + n for lo, n in CHUNKS].index(True)


def hops(m):
    return sum(min(v, 4 - v) for v in m)


def slot_of(u):
    return (u // 2, u % 2) if u < 2 * SELF else (u - SELF, None)


FAR_UNITS = sorted(range(2, UNITS), key=lambda u: -hops(PLACES[slot_of(u)[0]]))
FAR_CHIPS = sorted(ALL, key=lambda m: -hops(m))


def kernel(pts_hbm, tgt, ridge, coef_out, res_out, pts, bl, tl, tu, rr, qs1, qr1, qs2, qr2, ca, cb, cc,
           r_a, r_b, kt, ka, kb, sem_in, gb, gt, db, dt, sems, ack):
    me = lax.axis_index("pts")
    local = tgt.shape[1]
    dim = pts.shape[0]
    half = local // 2
    wide = 2 * dim
    core = lax.rem(me, 2)
    chip = me // 2
    pos = (chip // 16, lax.rem(chip // 4, 4), lax.rem(chip, 4))
    axis = [[lax.rem(pos[d] + a, 4) * (32, 8, 2)[d] for a in range(4)] for d in range(3)]
    cores = (core, 1 - core)
    upper = [p // 2 for p in pos]

    def device(m, c, sign=1):
        return sum(axis[d][sign * m[d] % 4] for d in range(3)) + c

    def split(s):
        return upper[PLACES[s].index(2)]

    partner = device((0, 0, 0), cores[1])
    load = pltpu.make_async_copy(pts_hbm, pts, sem_in)
    load.start()
    barrier = pltpu.get_barrier_semaphore()
    near = [partner] + [device(tuple(int(d == i) for i in range(3)), core, sign) for d in range(3) for sign in (1, -1)]
    for dev in near:
        pl.semaphore_signal(barrier, inc=1, device_id=(dev,), device_id_type=pl.DeviceIdType.MESH)

    target = tgt[...]
    tl[0, 0] = target
    tu[0] = target
    t_low = target.astype(BF16).astype(F32)

    load.wait()
    own_t = pts[...].astype(F32)
    own = own_t.T
    bl[0, 0] = jnp.concatenate([own[:half], own[half:]], axis=1).astype(BF16)

    def send(src, dst, ssem, rsem, dev):
        return pltpu.make_async_remote_copy(
            src_ref=src, dst_ref=dst, send_sem=ssem, recv_sem=rsem,
            device_id=(dev,), device_id_type=pl.DeviceIdType.MESH)

    def hop(s):
        _, src, d, sign = TREE[s - 1]
        g = chunk_of(s)
        dev = device(tuple(int(d == i) for i in range(3)), core, sign)
        return (send(bl.at[0, src], bl.at[0, s], sems.at[0], gb.at[g], dev),
                send(tl.at[0, src], tl.at[0, s], sems.at[1], gt.at[g], dev))

    def across_chip(s):
        g = chunk_of(s) if s else len(CHUNKS)
        return (send(bl.at[0, s], bl.at[1, s], sems.at[2], db.at[g], partner),
                send(tl.at[0, s], tl.at[1, s], sems.at[3], dt.at[g], partner))

    def start(copies):
        for copy in copies:
            copy.start()

    def arrive(plane, g):
        lo, n = CHUNKS[g] if g < len(CHUNKS) else (0, 1)
        for buf, sem in ((bl, (gb, db)[plane]), (tl, (gt, dt)[plane])):
            ref = buf.at[plane, pl.ds(lo, n)]
            send(ref, ref, sems.at[0], sem.at[g], partner).wait_recv()

    def serve(g):
        arrive(0, g)
        lo, n = CHUNKS[g]
        for s in range(1, SLOTS):
            if lo <= TREE[s - 1][1] < lo + n:
                start(hop(s))
        for s in range(lo, lo + n):
            start(across_chip(s))
        for s in range(lo, lo + n):
            pl.semaphore_signal(ack, inc=1, device_id=(device(PLACES[s], core, -1),), device_id_type=pl.DeviceIdType.MESH)

    def whole(buf, lo, sem):
        rest = buf.at[pl.ds(lo, buf.shape[0] - lo)]
        return send(rest, rest, sems.at[sem], sems.at[sem + 1], partner)

    def to_owner(qs, qr, sem, u):
        s, plane = slot_of(u)
        c = cores[plane] if plane is not None else lax.rem(core + split(s), 2)
        return send(qs.at[u], qr.at[u], sems.at[sem], sems.at[sem + 1], device(PLACES[s], c, -1))

    def to_user(buf, sem, u):
        s, plane = slot_of(u)
        c = cores[plane] if plane is not None else lax.rem(core + 1 + split(s), 2)
        return send(buf.at[0], buf.at[u], sems.at[sem], sems.at[sem + 1], device(PLACES[s], c))

    def to_all(buf, sem):
        for m in FAR_CHIPS:
            for p in (0, 1):
                if hops(m) + p:
                    at = p * 64 + m[0] * 16 + m[1] * 4 + m[2]
                    send(buf.at[0], buf.at[at], sems.at[sem], sems.at[sem + 1], device(m, cores[p])).start()

    pl.semaphore_wait(barrier, len(near))
    for s in range(1, SLOTS):
        if TREE[s - 1][1] == 0:
            start(hop(s))
    start(across_chip(0))

    s_row = jnp.sum(own_t * own_t, axis=0, keepdims=True) * (-1.0 / dim)
    s_hi = s_row.astype(BF16).astype(F32)
    s_mid = (s_row - s_hi).astype(BF16).astype(F32)
    s_lo = s_row - s_hi - s_mid
    rows = lax.broadcasted_iota(jnp.int32, (dim, local), 0)
    pieces = jnp.where(rows == 0, s_hi, jnp.where(rows == 1, s_mid, jnp.where(rows == 2, s_lo, 0.0)))
    pieces = pieces.astype(BF16)
    scaled = (own_t * (2.0 / dim)).astype(BF16)
    minus = jnp.full((dim, local), -1.0 / dim, BF16)
    r_a[0:dim] = scaled
    r_a[dim:2 * dim] = minus
    r_a[2 * dim:3 * dim] = minus
    r_a[3 * dim:4 * dim] = pieces
    r_b[0:dim] = minus
    r_b[dim:2 * dim] = scaled
    r_b[2 * dim:3 * dim] = pieces
    r_b[3 * dim:4 * dim] = minus

    lanes = lax.broadcasted_iota(jnp.int32, (half, wide), 1)
    first = lanes < dim
    one = jnp.ones((half, wide), BF16)

    def form(u, plane, s, keep):
        if not (isinstance(u, int) and u == 0):
            tu[u] = tl[plane, s]
        pb = bl[plane, s]
        f = pb.astype(F32)
        sq = f * f
        hi = sq.astype(BF16)
        lo = (sq - hi.astype(F32)).astype(BF16)
        hi = pltpu.roll(hi.astype(F32), dim, 1).astype(BF16)
        top = jnp.concatenate([jnp.where(first, pb, hi), jnp.where(first, lo, one)], axis=1)
        bot = jnp.concatenate([jnp.where(first, hi, pb), jnp.where(first, one, lo)], axis=1)
        for h, lhs, r in ((0, top, r_a), (1, bot, r_b)):
            e = jnp.dot(lhs, r[...], preferred_element_type=F32)
            k = jnp.exp(e).astype(BF16)
            kt[u, h * half:(h + 1) * half] = k
            keep[h * half:(h + 1) * half] = k

    def across(ks, weight):
        found = []
        for k in ks:
            x = k.astype(F32) * weight
            x = (x[:, :128] + x[:, 128:256]) + (x[:, 256:384] + x[:, 384:])
            found.append(jnp.sum(x.T, axis=0, keepdims=True))
        return jnp.concatenate(found, axis=1)

    def down(ks, v, acc):
        vb = v.astype(BF16)
        for h in (0, 1):
            acc = acc + jnp.dot(vb[:, h * half:(h + 1) * half], ks[h], preferred_element_type=F32)
        return acc

    def absorb(u, held, carry, factor=None):
        acc, tw = carry
        ks = [held[0:half], held[half:]]
        v = tu[u]
        q = across(ks, t_low)
        qs1[u] = q
        part = q * v
        if factor is not None:
            part = part * factor
        return down(ks, v, acc), tw + part

    zero = jnp.zeros((1, local), F32)
    form(0, 0, 0, ka)
    acc = down([ka[0:half], ka[half:]], target, zero)
    arrive(1, len(CHUNKS))
    form(1, 1, 0, kb)
    carry = (acc, zero)
    sent, ready = [], []

    def send_ready():
        for u in ready:
            to_owner(qs1, qr1, 8, u).start()
        sent.extend(ready)
        ready.clear()

    last = 1
    for g, (lo, n) in enumerate(CHUNKS):
        serve(g)
        send_ready()
        own_only = lo == SELF
        if own_only:
            arrive(1, g)

        def unit(f, lo=lo, n=n, own_only=own_only):
            if own_only:
                s = lo + f
                plane = split(lo)
                for i in range(1, n):
                    plane = jnp.where(f == i, split(lo + i), plane)
                return s + SELF, plane, s
            plane = jnp.where(f < n, 0, 1)
            s = lo + f - plane * n
            return 2 * s + plane, plane, s

        def two(i, carry, g=g, n=n, unit=unit, own_only=own_only, last=last):
            if not own_only:
                @pl.when(i == n // 2)
                def _():
                    arrive(1, g)

            a, b = unit(2 * i), unit(2 * i + 1)
            before = jnp.where(i == 0, last, unit(2 * i - 1)[0])
            factor = jnp.where(i == 0, 0.0, 1.0) if last == 1 else None
            carry = absorb(before, kb, carry, factor)
            form(*a, ka)
            carry = absorb(a[0], ka, carry)
            form(*b, kb)
            return carry

        carry = lax.fori_loop(0, n // 2 if own_only else n, two, carry)
        if last > 1:
            ready.append(last)
        if own_only:
            carry = absorb(lo + n - 2 + SELF, kb, carry)
            form(UNITS - 1, split(SLOTS - 1), SLOTS - 1, ka)
            carry = absorb(UNITS - 1, ka, carry)
            ready.extend(range(2 * SELF, UNITS))
        else:
            last = 2 * (lo + n - 1) + 1
            ready.extend(u for u in range(2 * lo, 2 * (lo + n)) if u != last)

    ready.reverse()
    send_ready()
    acc, tw = carry
    weight = ridge[0, 0]
    base = acc + weight * target
    lane = lax.broadcasted_iota(jnp.int32, (1, 128), 1)
    ca[0] = jnp.where(lane == 0, jnp.sum(tw + target * base), jnp.where(lane == 1, jnp.sum(target * target), 0.0))
    pl.semaphore_wait(ack, SLOTS - 1)
    to_all(ca, 6)
    moved = bl.at[0, pl.ds(1, SLOTS - 1)], tl.at[0, pl.ds(1, SLOTS - 1)], bl.at[0], tl.at[0]
    for i, ref in enumerate(moved):
        send(ref, ref, sems.at[i], sem_in, partner).wait_send()
    whole(qs1, 2, 8).wait_send()
    whole(qr1, 2, 8).wait_recv()
    w = base + jnp.sum(qr1[2:], axis=0)
    whole(ca, 1, 6).wait()
    sums = jnp.sum(ca[...], axis=0)
    norm0 = jnp.sum(sums[:, 1:2])
    step0 = norm0 / jnp.sum(sums[:, 0:1])
    r1 = target - step0 * w
    rr[0] = r1
    cb[0] = jnp.where(lane == 0, jnp.sum(r1 * r1), 0.0)
    for u in FAR_UNITS:
        to_user(rr, 10, u).start()
    send(rr.at[0], rr.at[1], sems.at[10], sems.at[11], partner).start()
    to_all(cb, 12)
    whole(rr, 1, 10).wait()
    whole(cb, 1, 12).wait()
    norm1 = jnp.sum(jnp.sum(cb[...], axis=0))
    beta = norm1 / norm0

    d_own = r1 + beta * target
    d_low = d_own.astype(BF16).astype(F32)

    def again(u):
        return [kt[u, 0:half], kt[u, half:]], rr[u] + beta * tu[u]

    acc = zero
    for u in (0, 1):
        acc = down(*again(u), acc)

    def second(u, carry):
        acc, curve = carry
        ks, v = again(u)
        q = across(ks, d_low)
        qs2[u] = q
        return down(ks, v, acc), curve + q * v

    carry = second(UNITS - 1, (acc, zero))
    edges = (UNITS - 2, UNITS - 24, UNITS - 44, 1)
    for hi, lo in zip(edges, edges[1:]):
        carry = lax.fori_loop(0, (hi - lo) // 2, lambda i, c, hi=hi: second(hi - 2 * i - 1, second(hi - 2 * i, c)), carry)
        for u in range(UNITS - 1 if hi == UNITS - 2 else hi, lo, -1):
            to_owner(qs2, qr2, 14, u).start()
    acc, curve = carry
    applied = acc + weight * d_own
    cc[0] = jnp.where(lane == 0, jnp.sum(d_own * applied + curve), 0.0)
    to_all(cc, 4)
    whole(qs2, 2, 14).wait_send()
    whole(qr2, 2, 14).wait_recv()
    applied = applied + jnp.sum(qr2[2:], axis=0)
    whole(cc, 1, 4).wait()
    step1 = norm1 / jnp.sum(jnp.sum(cc[...], axis=0))
    coef_out[...] = step0 * target + step1 * d_own
    res_out[...] = r1 - step1 * applied


def body(points, targets, ridge_weight):
    local, dim = points.shape
    half = local // 2
    dma = pltpu.SemaphoreType.DMA
    vec = jax.ShapeDtypeStruct((1, local), F32)
    rows = pltpu.VMEM((UNITS, 1, local), F32)
    small = pltpu.VMEM((128, 1, 128), F32)
    chunks = len(CHUNKS)
    coef, res = pl.pallas_call(
        kernel,
        out_shape=(vec, vec),
        in_specs=[
            pl.BlockSpec(memory_space=pl.ANY),
            pl.BlockSpec(memory_space=pltpu.VMEM),
            pl.BlockSpec(memory_space=pltpu.SMEM),
        ],
        out_specs=(pl.BlockSpec(memory_space=pltpu.VMEM), pl.BlockSpec(memory_space=pltpu.VMEM)),
        scratch_shapes=[
            pltpu.VMEM((dim, local), BF16),
            pltpu.VMEM((2, SLOTS, half, 2 * dim), BF16),
            pltpu.VMEM((2, SLOTS, 1, local), F32),
            rows, rows, rows, rows, rows, rows, small, small, small,
            pltpu.VMEM((4 * dim, local), BF16),
            pltpu.VMEM((4 * dim, local), BF16),
            pltpu.VMEM((UNITS, local, local), BF16),
            pltpu.VMEM((local, local), BF16),
            pltpu.VMEM((local, local), BF16),
            dma, dma((chunks,)), dma((chunks,)), dma((chunks + 1,)), dma((chunks + 1,)), dma((16,)),
            pltpu.SemaphoreType.REGULAR,
        ],
        compiler_params=pltpu.CompilerParams(
            collective_id=0, has_side_effects=True, vmem_limit_bytes=62 * 1024 * 1024),
    )(points.T, targets.reshape(1, local), ridge_weight.reshape(1, 1))
    return coef.reshape(local), res.reshape(local)


def solution(mesh):
    return jax.shard_map(
        body, mesh=mesh,
        in_specs=(P("pts", None), P("pts"), P()),
        out_specs=(P("pts"), P("pts")), check_vma=False)
```

time: 209 us -> 78 us (0.37)
  Pallas kernels: 204 us -> 74.5 us
    pallas_call x1, Pallas kernels: 204 us -> 74.5 us  [body(): pl.pallas_call(kernel, out_shape=(vec, vec), in_specs=[pl.BlockSpec(memor...]
where the time goes in v3:
time: 78 us; the launch traced here: 77.7 us
  Pallas kernels  74.5 us (96%)
  local copies, waits for them, and re-layouts  1.89 us (2%)
  between operations  1.29 us (2%)
    pallas_call x1, Pallas kernels, body(): pl.pallas_call(kernel, out_shape=(vec, vec), in_specs=[pl.BlockSpec(memor...  74.5 us
    unnamed x6, local copies, waits for them, and re-layouts  1.89 us

profile of v3, /device:TPU:1, one launch (start us, length us, event | category | flops | bytes accessed | tf_op | source)
XLA Modules:
  0.0 77.7 jit_solution(249674421976456562)
XLA Ops:
  1.3 74.5 %shard_map.50 = (f32[1,512]{1,0:T(1,128)}, f32[1,512]{1,0:T(1,128)}) custom-call(bf16[64,512]{1,0:T(8,128)(2,1)} %bitcast.6, f32[1,512]{1,0:T(1,128)} %bitcast.7, f32[1,1]{1,0:T(1,128)} %bitcast.5.ridge), custom_call_target="tpu_custom_call" | custom-call | tf_op jit(solution)/shard_map/pallas_call | solution.py:344
  75.8 0.0 copy-start.1
  75.8 0.7 copy-done.1
  76.5 0.0 copy-start
  76.5 0.6 copy.8
  77.1 0.1 copy-done
  77.1 0.6 copy.9
Async XLA Ops:
  75.8 0.7 copy-start.1
  76.5 0.7 copy-start

commit v4 on v3

--- a/solution.py
+++ b/solution.py
@@ -19,7 +19,8 @@
 SLOTS = len(PLACES)
 SELF = 29
 UNITS = 2 * SELF + SLOTS - SELF
-CHUNKS = ((1, 3), (4, 6), (10, 10), (20, 6), (26, 3), (SELF, SLOTS - SELF))
+CHUNKS = ((1, 3), (4, 6), (10, 10), (20, 6), (26, 3), (SELF, SLOTS - SELF - 1), (SLOTS - 1, 1))
+LOG2E = 1.4426950408889634
 ALL = tuple((z, y, x) for z in range(4) for y in range(4) for x in range(4))
 
 
@@ -39,13 +40,12 @@
 FAR_CHIPS = sorted(ALL, key=lambda m: -hops(m))
 
 
-def kernel(pts_hbm, tgt, ridge, coef_out, res_out, pts, bl, tl, tu, rr, qs1, qr1, qs2, qr2, ca, cb, cc,
-           r_a, r_b, kt, ka, kb, sem_in, gb, gt, db, dt, sems, ack):
+def kernel(pts_hbm, tgt, ridge, coef_out, res_out, bl, tl, tu, rr, qs1, qr1, qs2, qr2, ca, cb, cc,
+           own_l, pacc, kt, ka, kb, sem_in, gb, gt, db, dt, sems, ack):
     me = lax.axis_index("pts")
     local = tgt.shape[1]
-    dim = pts.shape[0]
+    dim = bl.shape[2]
     half = local // 2
-    wide = 2 * dim
     core = lax.rem(me, 2)
     chip = me // 2
     pos = (chip // 16, lax.rem(chip // 4, 4), lax.rem(chip, 4))
@@ -60,7 +60,7 @@
         return upper[PLACES[s].index(2)]
 
     partner = device((0, 0, 0), cores[1])
-    load = pltpu.make_async_copy(pts_hbm, pts, sem_in)
+    load = pltpu.make_async_copy(pts_hbm, bl.at[0, 0], sem_in)
     load.start()
     barrier = pltpu.get_barrier_semaphore()
     near = [partner] + [device(tuple(int(d == i) for i in range(3)), core, sign) for d in range(3) for sign in (1, -1)]
@@ -68,14 +68,12 @@
         pl.semaphore_signal(barrier, inc=1, device_id=(dev,), device_id_type=pl.DeviceIdType.MESH)
 
     target = tgt[...]
-    tl[0, 0] = target
-    tu[0] = target
-    t_low = target.astype(BF16).astype(F32)
+    t_bits = target.astype(BF16)
 
     load.wait()
-    own_t = pts[...].astype(F32)
-    own = own_t.T
-    bl[0, 0] = jnp.concatenate([own[:half], own[half:]], axis=1).astype(BF16)
+    own_t = bl[0, 0].astype(F32)
+    norm_row = jnp.sum(own_t * own_t, axis=0, keepdims=True) * (-LOG2E / dim)
+    tl[0, 0] = jnp.concatenate([target, norm_row], axis=1)
 
     def send(src, dst, ssem, rsem, dev):
         return pltpu.make_async_remote_copy(
@@ -142,76 +140,68 @@
             start(hop(s))
     start(across_chip(0))
 
-    s_row = jnp.sum(own_t * own_t, axis=0, keepdims=True) * (-1.0 / dim)
-    s_hi = s_row.astype(BF16).astype(F32)
-    s_mid = (s_row - s_hi).astype(BF16).astype(F32)
-    s_lo = s_row - s_hi - s_mid
-    rows = lax.broadcasted_iota(jnp.int32, (dim, local), 0)
-    pieces = jnp.where(rows == 0, s_hi, jnp.where(rows == 1, s_mid, jnp.where(rows == 2, s_lo, 0.0)))
-    pieces = pieces.astype(BF16)
-    scaled = (own_t * (2.0 / dim)).astype(BF16)
-    minus = jnp.full((dim, local), -1.0 / dim, BF16)
-    r_a[0:dim] = scaled
-    r_a[dim:2 * dim] = minus
-    r_a[2 * dim:3 * dim] = minus
-    r_a[3 * dim:4 * dim] = pieces
-    r_b[0:dim] = minus
-    r_b[dim:2 * dim] = scaled
-    r_b[2 * dim:3 * dim] = pieces
-    r_b[3 * dim:4 * dim] = minus
-
-    lanes = lax.broadcasted_iota(jnp.int32, (half, wide), 1)
-    first = lanes < dim
-    one = jnp.ones((half, wide), BF16)
+    def three(x):
+        hi = x.astype(BF16).astype(F32)
+        mid = (x - hi).astype(BF16).astype(F32)
+        return hi, mid, x - hi - mid
+
+    def tagged(lead, then):
+        rows = lax.broadcasted_iota(jnp.int32, (8, local), 0)
+        out = jnp.zeros((8, local), F32)
+        for i, x in enumerate(lead + then):
+            out = jnp.where(rows == i, x, out)
+        return jnp.concatenate([out, jnp.zeros((8, local), F32)], axis=0)
+
+    ones = (1.0, 1.0, 1.0)
+    left = jnp.concatenate([*three(own_t * (2.0 * LOG2E / dim)), tagged(ones, three(norm_row)),
+                            jnp.zeros((dim - 16, local), F32)], axis=0)
+    own_l[...] = left.T.astype(BF16)
+    rest = jnp.zeros((dim - 16, local), BF16)
 
     def form(u, plane, s, keep):
-        if not (isinstance(u, int) and u == 0):
-            tu[u] = tl[plane, s]
+        row = tl[plane, s]
+        tu[u] = row[:, :local]
         pb = bl[plane, s]
-        f = pb.astype(F32)
-        sq = f * f
-        hi = sq.astype(BF16)
-        lo = (sq - hi.astype(F32)).astype(BF16)
-        hi = pltpu.roll(hi.astype(F32), dim, 1).astype(BF16)
-        top = jnp.concatenate([jnp.where(first, pb, hi), jnp.where(first, lo, one)], axis=1)
-        bot = jnp.concatenate([jnp.where(first, hi, pb), jnp.where(first, one, lo)], axis=1)
-        for h, lhs, r in ((0, top, r_a), (1, bot, r_b)):
-            e = jnp.dot(lhs, r[...], preferred_element_type=F32)
-            k = jnp.exp(e).astype(BF16)
-            kt[u, h * half:(h + 1) * half] = k
-            keep[h * half:(h + 1) * half] = k
-
-    def across(ks, weight):
-        found = []
-        for k in ks:
-            x = k.astype(F32) * weight
-            x = (x[:, :128] + x[:, 128:256]) + (x[:, 256:384] + x[:, 384:])
-            found.append(jnp.sum(x.T, axis=0, keepdims=True))
-        return jnp.concatenate(found, axis=1)
-
-    def down(ks, v, acc):
-        vb = v.astype(BF16)
-        for h in (0, 1):
-            acc = acc + jnp.dot(vb[:, h * half:(h + 1) * half], ks[h], preferred_element_type=F32)
-        return acc
-
-    def absorb(u, held, carry, factor=None):
-        acc, tw = carry
-        ks = [held[0:half], held[half:]]
+        tags = tagged(three(row[:, local:]), ones).astype(BF16)
+        right = jnp.concatenate([pb, pb, pb, tags, rest], axis=0)
+        e = jnp.dot(own_l[...], right, preferred_element_type=F32)
+        k = jnp.exp2(e).astype(BF16)
+        kt[u] = k
+        keep[...] = k
+
+    def down(k, bits):
+        return jnp.dot(bits, k, preferred_element_type=F32)
+
+    def across(acc, *pairs):
+        lows = [v.astype(BF16).astype(F32) for _, v in pairs]
+        for r in range(0, local, 32):
+            cut = pl.ds(r, 32)
+            total = acc[cut]
+            for (k, _), low in zip(pairs, lows):
+                x = k[cut].astype(F32) * low
+                total = total + ((x[:, :128] + x[:, 128:256]) + (x[:, 256:384] + x[:, 384:]))
+            acc[cut] = total
+
+    def row_of():
+        return jnp.sum((pacc[0] + pacc[1]).T, axis=0, keepdims=True)
+
+    def absorb(u, side, tw, factor=None):
+        held = (ka, kb)[side]
         v = tu[u]
-        q = across(ks, t_low)
+        q = down(held[...], t_bits)
         qs1[u] = q
+        across(pacc.at[side], (held, v))
         part = q * v
         if factor is not None:
             part = part * factor
-        return down(ks, v, acc), tw + part
-
-    zero = jnp.zeros((1, local), F32)
+        return tw + part
+
+    pacc[...] = jnp.zeros_like(pacc)
     form(0, 0, 0, ka)
-    acc = down([ka[0:half], ka[half:]], target, zero)
+    across(pacc.at[0], (ka, target))
     arrive(1, len(CHUNKS))
     form(1, 1, 0, kb)
-    carry = (acc, zero)
+    tw = jnp.zeros((1, local), F32)
     sent, ready = [], []
 
     def send_ready():
@@ -220,57 +210,64 @@
         sent.extend(ready)
         ready.clear()
 
-    last = 1
-    for g, (lo, n) in enumerate(CHUNKS):
-        serve(g)
-        send_ready()
-        own_only = lo == SELF
-        if own_only:
-            arrive(1, g)
-
-        def unit(f, lo=lo, n=n, own_only=own_only):
-            if own_only:
-                s = lo + f
-                plane = split(lo)
-                for i in range(1, n):
-                    plane = jnp.where(f == i, split(lo + i), plane)
-                return s + SELF, plane, s
-            plane = jnp.where(f < n, 0, 1)
-            s = lo + f - plane * n
-            return 2 * s + plane, plane, s
-
-        def two(i, carry, g=g, n=n, unit=unit, own_only=own_only, last=last):
-            if not own_only:
+    def unit_of(g, f):
+        lo, n = CHUNKS[g]
+        if lo >= SELF:
+            plane = split(lo)
+            for i in range(1, n):
+                plane = jnp.where(f == i, split(lo + i), plane)
+            return lo + f + SELF, plane, lo + f
+        plane = jnp.where(f < n, 0, 1)
+        s = lo + f - plane * n
+        return 2 * s + plane, plane, s
+
+    def run(g, last, tw, factor=None):
+        lo, n = CHUNKS[g]
+
+        def two(i, tw):
+            if lo < SELF:
                 @pl.when(i == n // 2)
                 def _():
                     arrive(1, g)
 
-            a, b = unit(2 * i), unit(2 * i + 1)
-            before = jnp.where(i == 0, last, unit(2 * i - 1)[0])
-            factor = jnp.where(i == 0, 0.0, 1.0) if last == 1 else None
-            carry = absorb(before, kb, carry, factor)
+            a, b = unit_of(g, 2 * i), unit_of(g, 2 * i + 1)
+            before = jnp.where(i == 0, last, unit_of(g, 2 * i - 1)[0])
+            tw = absorb(before, 1, tw, None if last > 1 else jnp.where(i == 0, 0.0, 1.0))
             form(*a, ka)
-            carry = absorb(a[0], ka, carry)
+            tw = absorb(a[0], 0, tw)
             form(*b, kb)
-            return carry
-
-        carry = lax.fori_loop(0, n // 2 if own_only else n, two, carry)
+            return tw
+
+        tw = lax.fori_loop(0, n if lo < SELF else n // 2, two, tw)
+        units = [s + SELF for s in range(lo, lo + n)] if lo >= SELF else (
+            [2 * s for s in range(lo, lo + n)] + [2 * s + 1 for s in range(lo, lo + n)])
         if last > 1:
             ready.append(last)
-        if own_only:
-            carry = absorb(lo + n - 2 + SELF, kb, carry)
-            form(UNITS - 1, split(SLOTS - 1), SLOTS - 1, ka)
-            carry = absorb(UNITS - 1, ka, carry)
-            ready.extend(range(2 * SELF, UNITS))
-        else:
-            last = 2 * (lo + n - 1) + 1
-            ready.extend(u for u in range(2 * lo, 2 * (lo + n)) if u != last)
+        ready.extend(units[:-1])
+        return units[-1], tw
+
+    last = 1
+    for g in range(5):
+        serve(g)
+        send_ready()
+        if g < 4:
+            last, tw = run(g, last, tw)
+    serve(5)
+    arrive(1, 5)
+    last, tw = run(5, last, tw)
+    serve(6)
+    send_ready()
+    last, tw = run(4, last, tw)
+    arrive(1, 6)
+    tw = absorb(last, 1, tw)
+    form(UNITS - 1, split(SLOTS - 1), SLOTS - 1, ka)
+    tw = absorb(UNITS - 1, 0, tw)
+    ready.extend((last, UNITS - 1))
 
     ready.reverse()
     send_ready()
-    acc, tw = carry
     weight = ridge[0, 0]
-    base = acc + weight * target
+    base = row_of() + weight * target
     lane = lax.broadcasted_iota(jnp.int32, (1, 128), 1)
     ca[0] = jnp.where(lane == 0, jnp.sum(tw + target * base), jnp.where(lane == 1, jnp.sum(target * target), 0.0))
     pl.semaphore_wait(ack, SLOTS - 1)
@@ -298,30 +295,30 @@
     beta = norm1 / norm0
 
     d_own = r1 + beta * target
-    d_low = d_own.astype(BF16).astype(F32)
+    d_bits = d_own.astype(BF16)
+    pacc[...] = jnp.zeros_like(pacc)
 
     def again(u):
-        return [kt[u, 0:half], kt[u, half:]], rr[u] + beta * tu[u]
-
-    acc = zero
-    for u in (0, 1):
-        acc = down(*again(u), acc)
-
-    def second(u, carry):
-        acc, curve = carry
-        ks, v = again(u)
-        q = across(ks, d_low)
-        qs2[u] = q
-        return down(ks, v, acc), curve + q * v
-
-    carry = second(UNITS - 1, (acc, zero))
+        return kt.at[u], rr[u] + beta * tu[u]
+
+    across(pacc.at[0], again(0), again(1))
+
+    def second(curve, *units):
+        pairs = [again(u) for u in units]
+        for u, (k, v) in zip(units, pairs):
+            q = down(k[...], d_bits)
+            qs2[u] = q
+            curve = curve + q * v
+        across(pacc.at[0], *pairs)
+        return curve
+
+    curve = second(jnp.zeros((1, local), F32), UNITS - 1)
     edges = (UNITS - 2, UNITS - 24, UNITS - 44, 1)
     for hi, lo in zip(edges, edges[1:]):
-        carry = lax.fori_loop(0, (hi - lo) // 2, lambda i, c, hi=hi: second(hi - 2 * i - 1, second(hi - 2 * i, c)), carry)
+        curve = lax.fori_loop(0, (hi - lo) // 2, lambda i, c, hi=hi: second(c, hi - 2 * i, hi - 2 * i - 1), curve)
         for u in range(UNITS - 1 if hi == UNITS - 2 else hi, lo, -1):
             to_owner(qs2, qr2, 14, u).start()
-    acc, curve = carry
-    applied = acc + weight * d_own
+    applied = row_of() + weight * d_own
     cc[0] = jnp.where(lane == 0, jnp.sum(d_own * applied + curve), 0.0)
     to_all(cc, 4)
     whole(qs2, 2, 14).wait_send()
@@ -335,7 +332,6 @@
 
 def body(points, targets, ridge_weight):
     local, dim = points.shape
-    half = local // 2
     dma = pltpu.SemaphoreType.DMA
     vec = jax.ShapeDtypeStruct((1, local), F32)
     rows = pltpu.VMEM((UNITS, 1, local), F32)
@@ -351,12 +347,11 @@
         ],
         out_specs=(pl.BlockSpec(memory_space=pltpu.VMEM), pl.BlockSpec(memory_space=pltpu.VMEM)),
         scratch_shapes=[
-            pltpu.VMEM((dim, local), BF16),
-            pltpu.VMEM((2, SLOTS, half, 2 * dim), BF16),
-            pltpu.VMEM((2, SLOTS, 1, local), F32),
+            pltpu.VMEM((2, SLOTS, dim, local), BF16),
+            pltpu.VMEM((2, SLOTS, 1, 2 * local), F32),
             rows, rows, rows, rows, rows, rows, small, small, small,
-            pltpu.VMEM((4 * dim, local), BF16),
-            pltpu.VMEM((4 * dim, local), BF16),
+            pltpu.VMEM((local, 4 * dim), BF16),
+            pltpu.VMEM((2, local, 128), F32),
             pltpu.VMEM((UNITS, local, local), BF16),
             pltpu.VMEM((local, local), BF16),
             pltpu.VMEM((local, local), BF16),

time: 78 us -> 78.2 us (level)
  no operation moved by 1% of the time
where the time goes in v4:
time: 78.2 us; the launch traced here: 78 us
  Pallas kernels  74.8 us (96%)
  local copies, waits for them, and re-layouts  1.89 us (2%)
  between operations  1.29 us (2%)
    pallas_call x1, Pallas kernels, body(): pl.pallas_call(kernel, out_shape=(vec, vec), in_specs=[pl.BlockSpec(memor...  74.8 us
    unnamed x6, local copies, waits for them, and re-layouts  1.89 us

profile of v4, /device:TPU:1, one launch (start us, length us, event | category | flops | bytes accessed | tf_op | source)
XLA Modules:
  0.0 78.0 jit_solution(12218991273702797464)
XLA Ops:
  1.3 74.8 %shard_map.50 = (f32[1,512]{1,0:T(1,128)}, f32[1,512]{1,0:T(1,128)}) custom-call(bf16[64,512]{1,0:T(8,128)(2,1)} %bitcast.6, f32[1,512]{1,0:T(1,128)} %bitcast.7, f32[1,1]{1,0:T(1,128)} %bitcast.5.ridge), custom_call_target="tpu_custom_call" | custom-call | tf_op jit(solution)/shard_map/pallas_call | solution.py:340
  76.0 0.0 copy-start.1
  76.1 0.7 copy-done.1
  76.7 0.0 copy-start
  76.7 0.6 copy.8
  77.3 0.1 copy-done
  77.4 0.6 copy.9
Async XLA Ops:
  76.0 0.7 copy-start.1
  76.7 0.7 copy-start

commit v5 on v4

--- a/solution.py
+++ b/solution.py
@@ -19,8 +19,9 @@
 SLOTS = len(PLACES)
 SELF = 29
 UNITS = 2 * SELF + SLOTS - SELF
-CHUNKS = ((1, 3), (4, 6), (10, 10), (20, 6), (26, 3), (SELF, SLOTS - SELF - 1), (SLOTS - 1, 1))
+CHUNKS = ((1, 3), (4, 6), (10, 4), (14, 6), (20, 6), (26, 3), (SELF, SLOTS - SELF - 1), (SLOTS - 1, 1))
 LOG2E = 1.4426950408889634
+PLAN = ((0, (0,), 6), (1, (1,), 6), (2, (2,), 4), (3, (3, 4), 6), (4, (5,), 6), (6, (6,), 6), (5, (), 6))
 ALL = tuple((z, y, x) for z in range(4) for y in range(4) for x in range(4))
 
 
@@ -158,24 +159,27 @@
     own_l[...] = left.T.astype(BF16)
     rest = jnp.zeros((dim - 16, local), BF16)
 
-    def form(u, plane, s, keep):
+    def power(u, plane, s):
         row = tl[plane, s]
         tu[u] = row[:, :local]
         pb = bl[plane, s]
         tags = tagged(three(row[:, local:]), ones).astype(BF16)
         right = jnp.concatenate([pb, pb, pb, tags, rest], axis=0)
-        e = jnp.dot(own_l[...], right, preferred_element_type=F32)
-        k = jnp.exp2(e).astype(BF16)
-        kt[u] = k
-        keep[...] = k
+        return jnp.dot(own_l[...], right, preferred_element_type=F32)
+
+    def keep(u, e, side):
+        for r in range(0, local, 32):
+            k = jnp.exp2(e[r:r + 32]).astype(BF16)
+            kt[u, r:r + 32] = k
+            (ka, kb)[side][r:r + 32] = k
 
     def down(k, bits):
         return jnp.dot(bits, k, preferred_element_type=F32)
 
     def across(acc, *pairs):
         lows = [v.astype(BF16).astype(F32) for _, v in pairs]
-        for r in range(0, local, 32):
-            cut = pl.ds(r, 32)
+        for r in range(0, local, 16):
+            cut = pl.ds(r, 16)
             total = acc[cut]
             for (k, _), low in zip(pairs, lows):
                 x = k[cut].astype(F32) * low
@@ -197,10 +201,10 @@
         return tw + part
 
     pacc[...] = jnp.zeros_like(pacc)
-    form(0, 0, 0, ka)
+    keep(0, power(0, 0, 0), 0)
     across(pacc.at[0], (ka, target))
     arrive(1, len(CHUNKS))
-    form(1, 1, 0, kb)
+    keep(1, power(1, 1, 0), 1)
     tw = jnp.zeros((1, local), F32)
     sent, ready = [], []
 
@@ -221,24 +225,28 @@
         s = lo + f - plane * n
         return 2 * s + plane, plane, s
 
-    def run(g, last, tw, factor=None):
+    def run(g, last, tw, width):
         lo, n = CHUNKS[g]
-
-        def two(i, tw):
+        count = n if lo >= SELF else 2 * n
+
+        def some(i, tw):
             if lo < SELF:
-                @pl.when(i == n // 2)
+                @pl.when(i == n // width)
                 def _():
                     arrive(1, g)
 
-            a, b = unit_of(g, 2 * i), unit_of(g, 2 * i + 1)
-            before = jnp.where(i == 0, last, unit_of(g, 2 * i - 1)[0])
-            tw = absorb(before, 1, tw, None if last > 1 else jnp.where(i == 0, 0.0, 1.0))
-            form(*a, ka)
-            tw = absorb(a[0], 0, tw)
-            form(*b, kb)
+            units = [unit_of(g, width * i + j) for j in range(width)]
+            before = jnp.where(i == 0, last, unit_of(g, width * i - 1)[0])
+            factor = None if last > 1 else jnp.where(i == 0, 0.0, 1.0)
+            e = power(*units[0])
+            for j in range(width):
+                ahead = power(*units[j + 1]) if j + 1 < width else None
+                tw = absorb(units[j - 1][0] if j else before, 1 - j % 2, tw, None if j else factor)
+                keep(units[j][0], e, j % 2)
+                e = ahead
             return tw
 
-        tw = lax.fori_loop(0, n if lo < SELF else n // 2, two, tw)
+        tw = lax.fori_loop(0, count // width, some, tw)
         units = [s + SELF for s in range(lo, lo + n)] if lo >= SELF else (
             [2 * s for s in range(lo, lo + n)] + [2 * s + 1 for s in range(lo, lo + n)])
         if last > 1:
@@ -247,20 +255,18 @@
         return units[-1], tw
 
     last = 1
-    for g in range(5):
-        serve(g)
+    for g, then, width in PLAN:
+        for h in then:
+            serve(h)
+            if h >= 6:
+                arrive(1, h)
         send_ready()
-        if g < 4:
-            last, tw = run(g, last, tw)
-    serve(5)
-    arrive(1, 5)
-    last, tw = run(5, last, tw)
-    serve(6)
-    send_ready()
-    last, tw = run(4, last, tw)
-    arrive(1, 6)
+        last, tw = run(g, last, tw, width)
+    serve(7)
+    arrive(1, 7)
+    e = power(UNITS - 1, split(SLOTS - 1), SLOTS - 1)
     tw = absorb(last, 1, tw)
-    form(UNITS - 1, split(SLOTS - 1), SLOTS - 1, ka)
+    keep(UNITS - 1, e, 0)
     tw = absorb(UNITS - 1, 0, tw)
     ready.extend((last, UNITS - 1))
 

time: 78.2 us -> 79.5 us (1.017)
  Pallas kernels: 74.8 us -> 76.1 us
    pallas_call x1, Pallas kernels: 74.8 us -> 76.1 us  [body(): pl.pallas_call(kernel, out_shape=(vec, vec), in_specs=[pl.BlockSpec(memor...]
where the time goes in v5:
time: 79.5 us; the launch traced here: 79.3 us
  Pallas kernels  76.1 us (96%)
  local copies, waits for them, and re-layouts  1.89 us (2%)
  between operations  1.29 us (2%)
    pallas_call x1, Pallas kernels, body(): pl.pallas_call(kernel, out_shape=(vec, vec), in_specs=[pl.BlockSpec(memor...  76.1 us
    unnamed x6, local copies, waits for them, and re-layouts  1.89 us

profile of v5, /device:TPU:1, one launch (start us, length us, event | category | flops | bytes accessed | tf_op | source)
XLA Modules:
  0.0 79.3 jit_solution(14202252840316173290)
XLA Ops:
  1.3 76.1 %shard_map.50 = (f32[1,512]{1,0:T(1,128)}, f32[1,512]{1,0:T(1,128)}) custom-call(bf16[64,512]{1,0:T(8,128)(2,1)} %bitcast.6, f32[1,512]{1,0:T(1,128)} %bitcast.7, f32[1,1]{1,0:T(1,128)} %bitcast.5.ridge), custom_call_target="tpu_custom_call" | custom-call | tf_op jit(solution)/shard_map/pallas_call | solution.py:346
  77.4 0.0 copy-start.1
  77.4 0.7 copy-done.1
  78.0 0.0 copy-start
  78.0 0.6 copy.8
  78.6 0.1 copy-done
  78.7 0.6 copy.9
Async XLA Ops:
  77.4 0.7 copy-start.1
  78.0 0.7 copy-start

commit v6 on v5

--- a/solution.py
+++ b/solution.py
@@ -19,9 +19,27 @@
 SLOTS = len(PLACES)
 SELF = 29
 UNITS = 2 * SELF + SLOTS - SELF
-CHUNKS = ((1, 3), (4, 6), (10, 4), (14, 6), (20, 6), (26, 3), (SELF, SLOTS - SELF - 1), (SLOTS - 1, 1))
+CHUNKS = ((1, 3), (4, 6), (10, 10), (20, 6), (26, 3), (29, 3), (32, 3), (35, 1))
 LOG2E = 1.4426950408889634
-PLAN = ((0, (0,), 6), (1, (1,), 6), (2, (2,), 4), (3, (3, 4), 6), (4, (5,), 6), (6, (6,), 6), (5, (), 6))
+
+
+def plane_of(plane, lo, hi):
+    return tuple((s, plane) for s in range(lo, hi))
+
+
+PLAN = (
+    ((0,), (), plane_of(0, 1, 4)),
+    ((), (0,), plane_of(1, 1, 4)),
+    ((1,), (), plane_of(0, 4, 10)),
+    ((5,), (1,), plane_of(1, 4, 10)),
+    ((2,), (5,), plane_of(0, 10, 16)),
+    ((), (), plane_of(0, 16, 20) + plane_of(None, 29, 31)),
+    ((3,), (2,), plane_of(1, 10, 16)),
+    ((6,), (), plane_of(1, 16, 20) + plane_of(None, 31, 32)),
+    ((4,), (), plane_of(0, 20, 26)),
+    ((), (3, 6), plane_of(1, 20, 26)),
+    ((7,), (4,), plane_of(0, 26, 29) + plane_of(1, 26, 29)),
+    ((), (7,), plane_of(None, 32, 36)))
 ALL = tuple((z, y, x) for z in range(4) for y in range(4) for x in range(4))
 
 
@@ -37,6 +55,7 @@
     return (u // 2, u % 2) if u < 2 * SELF else (u - SELF, None)
 
 
+FAR = 40
 FAR_UNITS = sorted(range(2, UNITS), key=lambda u: -hops(PLACES[slot_of(u)[0]]))
 FAR_CHIPS = sorted(ALL, key=lambda m: -hops(m))
 
@@ -182,23 +201,22 @@
             cut = pl.ds(r, 16)
             total = acc[cut]
             for (k, _), low in zip(pairs, lows):
-                x = k[cut].astype(F32) * low
-                total = total + ((x[:, :128] + x[:, 128:256]) + (x[:, 256:384] + x[:, 384:]))
+                for c in range(0, local, 128):
+                    total = total + k[cut, c:c + 128].astype(F32) * low[:, c:c + 128]
             acc[cut] = total
 
     def row_of():
         return jnp.sum((pacc[0] + pacc[1]).T, axis=0, keepdims=True)
 
-    def absorb(u, side, tw, factor=None):
+    def absorb(u, side, tw):
         held = (ka, kb)[side]
         v = tu[u]
-        q = down(held[...], t_bits)
-        qs1[u] = q
+        q = None
+        if u > 1:
+            q = down(held[...], t_bits)
+            qs1[u] = q
         across(pacc.at[side], (held, v))
-        part = q * v
-        if factor is not None:
-            part = part * factor
-        return tw + part
+        return tw if q is None else tw + q * v
 
     pacc[...] = jnp.zeros_like(pacc)
     keep(0, power(0, 0, 0), 0)
@@ -214,61 +232,26 @@
         sent.extend(ready)
         ready.clear()
 
-    def unit_of(g, f):
-        lo, n = CHUNKS[g]
-        if lo >= SELF:
-            plane = split(lo)
-            for i in range(1, n):
-                plane = jnp.where(f == i, split(lo + i), plane)
-            return lo + f + SELF, plane, lo + f
-        plane = jnp.where(f < n, 0, 1)
-        s = lo + f - plane * n
-        return 2 * s + plane, plane, s
-
-    def run(g, last, tw, width):
-        lo, n = CHUNKS[g]
-        count = n if lo >= SELF else 2 * n
-
-        def some(i, tw):
-            if lo < SELF:
-                @pl.when(i == n // width)
-                def _():
-                    arrive(1, g)
-
-            units = [unit_of(g, width * i + j) for j in range(width)]
-            before = jnp.where(i == 0, last, unit_of(g, width * i - 1)[0])
-            factor = None if last > 1 else jnp.where(i == 0, 0.0, 1.0)
-            e = power(*units[0])
-            for j in range(width):
-                ahead = power(*units[j + 1]) if j + 1 < width else None
-                tw = absorb(units[j - 1][0] if j else before, 1 - j % 2, tw, None if j else factor)
-                keep(units[j][0], e, j % 2)
-                e = ahead
-            return tw
-
-        tw = lax.fori_loop(0, count // width, some, tw)
-        units = [s + SELF for s in range(lo, lo + n)] if lo >= SELF else (
-            [2 * s for s in range(lo, lo + n)] + [2 * s + 1 for s in range(lo, lo + n)])
-        if last > 1:
-            ready.append(last)
-        ready.extend(units[:-1])
-        return units[-1], tw
-
-    last = 1
-    for g, then, width in PLAN:
-        for h in then:
-            serve(h)
-            if h >= 6:
-                arrive(1, h)
+    prev, count = 1, 1
+    for served, crossed, units in PLAN:
+        for g in served:
+            serve(g)
+        for g in crossed:
+            arrive(1, g)
         send_ready()
-        last, tw = run(g, last, tw, width)
-    serve(7)
-    arrive(1, 7)
-    e = power(UNITS - 1, split(SLOTS - 1), SLOTS - 1)
-    tw = absorb(last, 1, tw)
-    keep(UNITS - 1, e, 0)
-    tw = absorb(UNITS - 1, 0, tw)
-    ready.extend((last, UNITS - 1))
+        units = [(s + SELF, split(s), s) if plane is None else (2 * s + plane, plane, s) for s, plane in units]
+        e = power(*units[0])
+        for j, (u, _, _) in enumerate(units):
+            ahead = power(*units[j + 1]) if j + 1 < len(units) else None
+            tw = absorb(prev, count % 2, tw)
+            if prev > 1:
+                ready.append(prev)
+            count += 1
+            keep(u, e, count % 2)
+            prev, e = u, ahead
+
+    tw = absorb(prev, count % 2, tw)
+    ready.append(prev)
 
     ready.reverse()
     send_ready()
@@ -291,14 +274,14 @@
     r1 = target - step0 * w
     rr[0] = r1
     cb[0] = jnp.where(lane == 0, jnp.sum(r1 * r1), 0.0)
+    to_all(cb, 12)
     for u in FAR_UNITS:
-        to_user(rr, 10, u).start()
+        to_user(rr, 16 if u >= FAR else 10, u).start()
     send(rr.at[0], rr.at[1], sems.at[10], sems.at[11], partner).start()
-    to_all(cb, 12)
-    whole(rr, 1, 10).wait()
     whole(cb, 1, 12).wait()
     norm1 = jnp.sum(jnp.sum(cb[...], axis=0))
     beta = norm1 / norm0
+    whole(rr.at[pl.ds(0, FAR)], 1, 10).wait()
 
     d_own = r1 + beta * target
     d_bits = d_own.astype(BF16)
@@ -311,18 +294,22 @@
 
     def second(curve, *units):
         pairs = [again(u) for u in units]
+        across(pacc.at[0], *pairs)
         for u, (k, v) in zip(units, pairs):
             q = down(k[...], d_bits)
             qs2[u] = q
             curve = curve + q * v
-        across(pacc.at[0], *pairs)
         return curve
 
-    curve = second(jnp.zeros((1, local), F32), UNITS - 1)
-    edges = (UNITS - 2, UNITS - 24, UNITS - 44, 1)
-    for hi, lo in zip(edges, edges[1:]):
-        curve = lax.fori_loop(0, (hi - lo) // 2, lambda i, c, hi=hi: second(c, hi - 2 * i, hi - 2 * i - 1), curve)
-        for u in range(UNITS - 1 if hi == UNITS - 2 else hi, lo, -1):
+    curve = jnp.zeros((1, local), F32)
+    curve = lax.fori_loop(1, FAR // 2, lambda i, c: second(c, 2 * i, 2 * i + 1), curve)
+    for u in range(2, FAR):
+        to_owner(qs2, qr2, 14, u).start()
+    whole(rr, FAR, 16).wait()
+    curve = lax.fori_loop(FAR // 2, UNITS // 2, lambda i, c: second(c, 2 * i, 2 * i + 1), curve)
+    curve = second(curve, UNITS - 1)
+    for u in FAR_UNITS:
+        if u >= FAR:
             to_owner(qs2, qr2, 14, u).start()
     applied = row_of() + weight * d_own
     cc[0] = jnp.where(lane == 0, jnp.sum(d_own * applied + curve), 0.0)
@@ -361,7 +348,7 @@
             pltpu.VMEM((UNITS, local, local), BF16),
             pltpu.VMEM((local, local), BF16),
             pltpu.VMEM((local, local), BF16),
-            dma, dma((chunks,)), dma((chunks,)), dma((chunks + 1,)), dma((chunks + 1,)), dma((16,)),
+            dma, dma((chunks,)), dma((chunks,)), dma((chunks + 1,)), dma((chunks + 1,)), dma((18,)),
             pltpu.SemaphoreType.REGULAR,
         ],
         compiler_params=pltpu.CompilerParams(

time: 79.5 us -> 74.6 us (0.938)
  Pallas kernels: 76.1 us -> 71.2 us
    pallas_call x1, Pallas kernels: 76.1 us -> 71.2 us  [body(): pl.pallas_call(kernel, out_shape=(vec, vec), in_specs=[pl.BlockSpec(memor...]
where the time goes in v6:
time: 74.6 us; the launch traced here: 74.4 us
  Pallas kernels  71.2 us (95%)
  local copies, waits for them, and re-layouts  1.89 us (3%)
  between operations  1.29 us (2%)
    pallas_call x1, Pallas kernels, body(): pl.pallas_call(kernel, out_shape=(vec, vec), in_specs=[pl.BlockSpec(memor...  71.2 us
    unnamed x6, local copies, waits for them, and re-layouts  1.89 us

profile of v6, /device:TPU:1, one launch (start us, length us, event | category | flops | bytes accessed | tf_op | source)
XLA Modules:
  0.0 74.4 jit_solution(9560639580842856270)
XLA Ops:
  1.3 71.2 %shard_map.50 = (f32[1,512]{1,0:T(1,128)}, f32[1,512]{1,0:T(1,128)}) custom-call(bf16[64,512]{1,0:T(8,128)(2,1)} %bitcast.6, f32[1,512]{1,0:T(1,128)} %bitcast.7, f32[1,1]{1,0:T(1,128)} %bitcast.5.ridge), custom_call_target="tpu_custom_call" | custom-call | tf_op jit(solution)/shard_map/pallas_call | solution.py:333
  72.5 0.0 copy-start.1
  72.5 0.7 copy-done.1
  73.1 0.0 copy-start
  73.1 0.6 copy.8
  73.7 0.1 copy-done
  73.8 0.6 copy.9
Async XLA Ops:
  72.5 0.7 copy-start.1
  73.1 0.7 copy-start

commit v7 on v6

--- a/solution.py
+++ b/solution.py
@@ -55,15 +55,17 @@
     return (u // 2, u % 2) if u < 2 * SELF else (u - SELF, None)
 
 
+TOP = 384
+WIDTH = 4
 FAR = 40
 FAR_UNITS = sorted(range(2, UNITS), key=lambda u: -hops(PLACES[slot_of(u)[0]]))
 FAR_CHIPS = sorted(ALL, key=lambda m: -hops(m))
 
 
-def kernel(pts_hbm, tgt, ridge, coef_out, res_out, bl, tl, tu, rr, qs1, qr1, qs2, qr2, ca, cb, cc,
+def kernel(pts_hbm, tgt_hbm, ridge, coef_out, res_out, tgt, bl, tl, tu, rr, qs1, qr1, qs2, qr2, ca, cb, cc,
            own_l, pacc, kt, ka, kb, sem_in, gb, gt, db, dt, sems, ack):
     me = lax.axis_index("pts")
-    local = tgt.shape[1]
+    local = tgt_hbm.shape[1]
     dim = bl.shape[2]
     half = local // 2
     core = lax.rem(me, 2)
@@ -82,11 +84,14 @@
     partner = device((0, 0, 0), cores[1])
     load = pltpu.make_async_copy(pts_hbm, bl.at[0, 0], sem_in)
     load.start()
+    fetch = pltpu.make_async_copy(tgt_hbm, tgt, sems.at[0])
+    fetch.start()
     barrier = pltpu.get_barrier_semaphore()
     near = [partner] + [device(tuple(int(d == i) for i in range(3)), core, sign) for d in range(3) for sign in (1, -1)]
     for dev in near:
         pl.semaphore_signal(barrier, inc=1, device_id=(dev,), device_id_type=pl.DeviceIdType.MESH)
 
+    fetch.wait()
     target = tgt[...]
     t_bits = target.astype(BF16)
 
@@ -125,11 +130,11 @@
     def serve(g):
         arrive(0, g)
         lo, n = CHUNKS[g]
+        for s in range(lo, lo + n):
+            start(across_chip(s))
         for s in range(1, SLOTS):
             if lo <= TREE[s - 1][1] < lo + n:
                 start(hop(s))
-        for s in range(lo, lo + n):
-            start(across_chip(s))
         for s in range(lo, lo + n):
             pl.semaphore_signal(ack, inc=1, device_id=(device(PLACES[s], core, -1),), device_id_type=pl.DeviceIdType.MESH)
 
@@ -195,9 +200,9 @@
     def down(k, bits):
         return jnp.dot(bits, k, preferred_element_type=F32)
 
-    def across(acc, *pairs):
+    def across(acc, *pairs, rows=None):
         lows = [v.astype(BF16).astype(F32) for _, v in pairs]
-        for r in range(0, local, 16):
+        for r in range(0, rows or local, 16):
             cut = pl.ds(r, 16)
             total = acc[cut]
             for (k, _), low in zip(pairs, lows):
@@ -292,26 +297,34 @@
 
     across(pacc.at[0], again(0), again(1))
 
-    def second(curve, *units):
+    def second(carry, *units):
+        curve, tail = carry
         pairs = [again(u) for u in units]
-        across(pacc.at[0], *pairs)
+        for k, v in pairs:
+            tail = tail + lax.dot_general(v.astype(BF16), k[TOP:], (((1,), (1,)), ((), ())), preferred_element_type=F32)
+        across(pacc.at[0], *pairs, rows=TOP)
         for u, (k, v) in zip(units, pairs):
             q = down(k[...], d_bits)
             qs2[u] = q
             curve = curve + q * v
-        return curve
-
-    curve = jnp.zeros((1, local), F32)
-    curve = lax.fori_loop(1, FAR // 2, lambda i, c: second(c, 2 * i, 2 * i + 1), curve)
+        return curve, tail
+
+    def seconds(carry, lo, hi):
+        steps = (hi - lo) // WIDTH
+        carry = lax.fori_loop(0, steps, lambda i, c: second(c, *(lo + WIDTH * i + j for j in range(WIDTH))), carry)
+        rest = range(lo + WIDTH * steps, hi)
+        return second(carry, *rest) if rest else carry
+
+    carry = (jnp.zeros((1, local), F32), jnp.zeros((1, local - TOP), F32))
+    carry = seconds(carry, 2, FAR)
     for u in range(2, FAR):
         to_owner(qs2, qr2, 14, u).start()
     whole(rr, FAR, 16).wait()
-    curve = lax.fori_loop(FAR // 2, UNITS // 2, lambda i, c: second(c, 2 * i, 2 * i + 1), curve)
-    curve = second(curve, UNITS - 1)
+    curve, tail = seconds(carry, FAR, UNITS)
     for u in FAR_UNITS:
         if u >= FAR:
             to_owner(qs2, qr2, 14, u).start()
-    applied = row_of() + weight * d_own
+    applied = row_of() + jnp.concatenate([jnp.zeros((1, TOP), F32), tail], axis=1) + weight * d_own
     cc[0] = jnp.where(lane == 0, jnp.sum(d_own * applied + curve), 0.0)
     to_all(cc, 4)
     whole(qs2, 2, 14).wait_send()
@@ -319,14 +332,14 @@
     applied = applied + jnp.sum(qr2[2:], axis=0)
     whole(cc, 1, 4).wait()
     step1 = norm1 / jnp.sum(jnp.sum(cc[...], axis=0))
-    coef_out[...] = step0 * target + step1 * d_own
-    res_out[...] = r1 - step1 * applied
+    coef_out[...] = (step0 * target + step1 * d_own).reshape(local)
+    res_out[...] = (r1 - step1 * applied).reshape(local)
 
 
 def body(points, targets, ridge_weight):
     local, dim = points.shape
     dma = pltpu.SemaphoreType.DMA
-    vec = jax.ShapeDtypeStruct((1, local), F32)
+    vec = jax.ShapeDtypeStruct((local,), F32)
     rows = pltpu.VMEM((UNITS, 1, local), F32)
     small = pltpu.VMEM((128, 1, 128), F32)
     chunks = len(CHUNKS)
@@ -335,11 +348,12 @@
         out_shape=(vec, vec),
         in_specs=[
             pl.BlockSpec(memory_space=pl.ANY),
-            pl.BlockSpec(memory_space=pltpu.VMEM),
+            pl.BlockSpec(memory_space=pl.ANY),
             pl.BlockSpec(memory_space=pltpu.SMEM),
         ],
         out_specs=(pl.BlockSpec(memory_space=pltpu.VMEM), pl.BlockSpec(memory_space=pltpu.VMEM)),
         scratch_shapes=[
+            pltpu.VMEM((1, local), F32),
             pltpu.VMEM((2, SLOTS, dim, local), BF16),
             pltpu.VMEM((2, SLOTS, 1, 2 * local), F32),
             rows, rows, rows, rows, rows, rows, small, small, small,
@@ -354,7 +368,7 @@
         compiler_params=pltpu.CompilerParams(
             collective_id=0, has_side_effects=True, vmem_limit_bytes=62 * 1024 * 1024),
     )(points.T, targets.reshape(1, local), ridge_weight.reshape(1, 1))
-    return coef.reshape(local), res.reshape(local)
+    return coef, res
 
 
 def solution(mesh):

time: 74.6 us -> 73.2 us (0.981)
  Pallas kernels: 71.2 us -> 69.8 us
    pallas_call x1, Pallas kernels: 71.2 us -> 69.8 us  [body(): pl.pallas_call(kernel, out_shape=(vec, vec), in_specs=[pl.BlockSpec(memor...]
where the time goes in v7:
time: 73.2 us; the launch traced here: 73 us
  Pallas kernels  69.8 us (95%)
  local copies, waits for them, and re-layouts  1.89 us (3%)
  between operations  1.29 us (2%)
    pallas_call x1, Pallas kernels, body(): pl.pallas_call(kernel, out_shape=(vec, vec), in_specs=[pl.BlockSpec(memor...  69.8 us
    unnamed x6, local copies, waits for them, and re-layouts  1.89 us

profile of v7, /device:TPU:1, one launch (start us, length us, event | category | flops | bytes accessed | tf_op | source)
XLA Modules:
  0.0 73.0 jit_solution(1606165000896348823)
XLA Ops:
  1.3 69.8 %shard_map.50 = (f32[512]{0:T(512)}, f32[512]{0:T(512)}) custom-call(bf16[64,512]{1,0:T(8,128)(2,1)} %bitcast.4, f32[1,512]{1,0:T(1,128)} %bitcast.5, f32[1,1]{1,0:T(1,128)} %bitcast.3.ridge), custom_call_target="tpu_custom_call" | custom-call | tf_op jit(solution)/shard_map/pallas_call | solution.py:346
  71.1 0.0 copy-start.1
  71.1 0.7 copy-done.1
  71.8 0.0 copy-start
  71.8 0.6 copy.8
  72.4 0.1 copy-done
  72.4 0.6 copy.9
Async XLA Ops:
  71.1 0.7 copy-start.1
  71.8 0.7 copy-start

commit v8 on v7

--- a/solution.py
+++ b/solution.py
@@ -135,7 +135,7 @@
         for s in range(1, SLOTS):
             if lo <= TREE[s - 1][1] < lo + n:
                 start(hop(s))
-        for s in range(lo, lo + n):
+        for s in range(lo, min(lo + n, SELF)):
             pl.semaphore_signal(ack, inc=1, device_id=(device(PLACES[s], core, -1),), device_id_type=pl.DeviceIdType.MESH)
 
     def whole(buf, lo, sem):
@@ -264,7 +264,7 @@
     base = row_of() + weight * target
     lane = lax.broadcasted_iota(jnp.int32, (1, 128), 1)
     ca[0] = jnp.where(lane == 0, jnp.sum(tw + target * base), jnp.where(lane == 1, jnp.sum(target * target), 0.0))
-    pl.semaphore_wait(ack, SLOTS - 1)
+    pl.semaphore_wait(ack, SELF - 1)
     to_all(ca, 6)
     moved = bl.at[0, pl.ds(1, SLOTS - 1)], tl.at[0, pl.ds(1, SLOTS - 1)], bl.at[0], tl.at[0]
     for i, ref in enumerate(moved):

time: 73.2 us -> 72.3 us (0.988)
  Pallas kernels: 69.8 us -> 68.9 us
    pallas_call x1, Pallas kernels: 69.8 us -> 68.9 us  [body(): pl.pallas_call(kernel, out_shape=(vec, vec), in_specs=[pl.BlockSpec(memor...]
where the time goes in v8:
time: 72.3 us; the launch traced here: 72.1 us
  Pallas kernels  68.9 us (95%)
  local copies, waits for them, and re-layouts  1.89 us (3%)
  between operations  1.29 us (2%)
    pallas_call x1, Pallas kernels, body(): pl.pallas_call(kernel, out_shape=(vec, vec), in_specs=[pl.BlockSpec(memor...  68.9 us
    unnamed x6, local copies, waits for them, and re-layouts  1.89 us

profile of v8, /device:TPU:1, one launch (start us, length us, event | category | flops | bytes accessed | tf_op | source)
XLA Modules:
  0.0 72.1 jit_solution(684146491829425507)
XLA Ops:
  1.3 68.9 %shard_map.50 = (f32[512]{0:T(512)}, f32[512]{0:T(512)}) custom-call(bf16[64,512]{1,0:T(8,128)(2,1)} %bitcast.4, f32[1,512]{1,0:T(1,128)} %bitcast.5, f32[1,1]{1,0:T(1,128)} %bitcast.3.ridge), custom_call_target="tpu_custom_call" | custom-call | tf_op jit(solution)/shard_map/pallas_call | solution.py:346
  70.2 0.0 copy-start.1
  70.2 0.7 copy-done.1
  70.9 0.0 copy-start
  70.9 0.6 copy.8
  71.4 0.1 copy-done
  71.5 0.6 copy.9
Async XLA Ops:
  70.2 0.7 copy-start.1
  70.9 0.7 copy-start

commit v9 on v8

--- a/solution.py
+++ b/solution.py
@@ -38,8 +38,9 @@
     ((6,), (), plane_of(1, 16, 20) + plane_of(None, 31, 32)),
     ((4,), (), plane_of(0, 20, 26)),
     ((), (3, 6), plane_of(1, 20, 26)),
-    ((7,), (4,), plane_of(0, 26, 29) + plane_of(1, 26, 29)),
-    ((), (7,), plane_of(None, 32, 36)))
+    ((7,), (), plane_of(0, 26, 29) + plane_of(None, 32, 35)),
+    ((), (4,), plane_of(1, 26, 29)),
+    ((), (7,), plane_of(None, 35, 36)))
 ALL = tuple((z, y, x) for z in range(4) for y in range(4) for x in range(4))
 
 

time: 72.3 us -> 72.5 us (level)
  no operation moved by 1% of the time
where the time goes in v9:
time: 72.5 us; the launch traced here: 72.3 us
  Pallas kernels  69.1 us (95%)
  local copies, waits for them, and re-layouts  1.89 us (3%)
  between operations  1.29 us (2%)
    pallas_call x1, Pallas kernels, body(): pl.pallas_call(kernel, out_shape=(vec, vec), in_specs=[pl.BlockSpec(memor...  69.1 us
    unnamed x6, local copies, waits for them, and re-layouts  1.89 us

profile of v9, /device:TPU:1, one launch (start us, length us, event | category | flops | bytes accessed | tf_op | source)
XLA Modules:
  0.0 72.3 jit_solution(15396034457399024166)
XLA Ops:
  1.3 69.1 %shard_map.50 = (f32[512]{0:T(512)}, f32[512]{0:T(512)}) custom-call(bf16[64,512]{1,0:T(8,128)(2,1)} %bitcast.4, f32[1,512]{1,0:T(1,128)} %bitcast.5, f32[1,1]{1,0:T(1,128)} %bitcast.3.ridge), custom_call_target="tpu_custom_call" | custom-call | tf_op jit(solution)/shard_map/pallas_call | solution.py:347
  70.4 0.0 copy-start.1
  70.4 0.7 copy-done.1
  71.0 0.0 copy-start
  71.0 0.6 copy.8
  71.6 0.1 copy-done
  71.7 0.6 copy.9
Async XLA Ops:
  70.4 0.7 copy-start.1
  71.0 0.7 copy-start

commit v10 on v8

--- a/solution.py
+++ b/solution.py
@@ -28,7 +28,7 @@
 
 
 PLAN = (
-    ((0,), (), plane_of(0, 1, 4)),
+    ((0,), (len(CHUNKS),), plane_of(0, 1, 4) + plane_of(0, 0, 1) + plane_of(1, 0, 1)),
     ((), (0,), plane_of(1, 1, 4)),
     ((1,), (), plane_of(0, 4, 10)),
     ((5,), (1,), plane_of(1, 4, 10)),
@@ -224,10 +224,6 @@
         return tw if q is None else tw + q * v
 
     pacc[...] = jnp.zeros_like(pacc)
-    keep(0, power(0, 0, 0), 0)
-    across(pacc.at[0], (ka, target))
-    arrive(1, len(CHUNKS))
-    keep(1, power(1, 1, 0), 1)
     tw = jnp.zeros((1, local), F32)
     sent, ready = [], []
 
@@ -237,7 +233,7 @@
         sent.extend(ready)
         ready.clear()
 
-    prev, count = 1, 1
+    prev, count = None, 1
     for served, crossed, units in PLAN:
         for g in served:
             serve(g)
@@ -248,9 +244,10 @@
         e = power(*units[0])
         for j, (u, _, _) in enumerate(units):
             ahead = power(*units[j + 1]) if j + 1 < len(units) else None
-            tw = absorb(prev, count % 2, tw)
-            if prev > 1:
-                ready.append(prev)
+            if prev is not None:
+                tw = absorb(prev, count % 2, tw)
+                if prev > 1:
+                    ready.append(prev)
             count += 1
             keep(u, e, count % 2)
             prev, e = u, ahead

time: 72.3 us -> 72.3 us (level)
  no operation moved by 1% of the time
where the time goes in v10:
time: 72.3 us; the launch traced here: 72.1 us
  Pallas kernels  68.9 us (95%)
  local copies, waits for them, and re-layouts  1.89 us (3%)
  between operations  1.29 us (2%)
    pallas_call x1, Pallas kernels, body(): pl.pallas_call(kernel, out_shape=(vec, vec), in_specs=[pl.BlockSpec(memor...  68.9 us
    unnamed x6, local copies, waits for them, and re-layouts  1.89 us

profile of v10, /device:TPU:1, one launch (start us, length us, event | category | flops | bytes accessed | tf_op | source)
XLA Modules:
  0.0 72.1 jit_solution(16766635169415919844)
XLA Ops:
  1.3 68.9 %shard_map.50 = (f32[512]{0:T(512)}, f32[512]{0:T(512)}) custom-call(bf16[64,512]{1,0:T(8,128)(2,1)} %bitcast.4, f32[1,512]{1,0:T(1,128)} %bitcast.5, f32[1,1]{1,0:T(1,128)} %bitcast.3.ridge), custom_call_target="tpu_custom_call" | custom-call | tf_op jit(solution)/shard_map/pallas_call | solution.py:343
  70.2 0.0 copy-start.1
  70.2 0.7 copy-done.1
  70.8 0.0 copy-start
  70.9 0.6 copy.8
  71.4 0.1 copy-done
  71.5 0.6 copy.9
Async XLA Ops:
  70.2 0.7 copy-start.1
  70.8 0.7 copy-start
